TPU v7x, 768 devices: a whole 4x8x12 slice. The times are simulated.
768 devices in a mesh: dp: 16 (over x, z_lo), expert: 8 (over y), tensor: 6 (over z_hi, core).
Axes of the slice: x: 4, y: 8, z: 12 (z_hi: 3, z_lo: 4; z = z_hi * 4 + z_lo), core: 2. Of those that a mesh axis runs over, the one named last changes fastest.
Arguments:
- tokens: bfloat16 [2048, 6144], P('dp'), may hold values from -6 to 6
- norm_gain: float32 [6144], replicated, may hold values from 0.1 to 1.9
- expert_ids: int32 [2048, 2], P('dp'), may hold values from 0 to 7, all different within a row; in each aligned block of 128 rows (0 to 127, 128 to 255, ...) at most 36 rows name the same one
- gate_weights: float32 [2048, 2], P('dp'), may hold values from 0.1 to 0.9
- w_gate: bfloat16 [8, 6144, 12288], P('expert', None, ('dp', 'tensor')), may hold values from -0.078125 to 0.078125
- w_up: bfloat16 [8, 6144, 12288], P('expert', None, ('dp', 'tensor')), may hold values from -0.078125 to 0.078125
- w_down: bfloat16 [8, 12288, 6144], P('expert', 'dp', 'tensor'), may hold values from -0.0546875 to 0.0546875
- label_rows: bfloat16 [2048, 6144], P(('dp', 'expert'), 'tensor'), may hold values from -4 to 4, as said below
- seg_ids: int32 [16, 128], P('dp'), may hold values from 0 to 3, never falling along the last dimension, each value on 1 to 64 neighbouring positions
- pair_slot: int32 [16, 4], P('dp'), may hold values from 0 to 3, each once within a row
- ref_scores: float32 [16, 4], P('dp'), may hold values from -8 to 8
Outputs:
- layer_out: bfloat16 [2048, 6144], P(('dp', 'expert'), 'tensor')
- margins: float32 [16, 2], P('dp')
Inputs may be any that keep to these rules, and one draw needn't show every extreme that they name: `expert_ids`: each row names two different experts. Among the 128 rows of one dp group no expert is named more than 36 times, and in some group some expert is named exactly 36 times. `seg_ids`: within each row sequence numbers never fall; every sequence has 1 to 64 tokens and one has exactly 64. `pair_slot`: each row holds every number of 0 to 3 once. `label_rows`: entries lie within 27 / sqrt(6144) in magnitude.
All inputs are finite; a program needn't handle non-finite values.
Results may differ from a plain program's by a relative error of at most 0.009.
Values may be sent and summed in bfloat16 or wider, within the bound.
No kernel may reach another device: no remote copies, remote signals or barrier semaphores. Data moves between devices by JAX's collectives and lax.ppermute only.
A program may use at most 64 MiB of HBM per device.

v0:
```python
import functools

import jax
import jax.numpy as jnp
from jax import lax
from jax.experimental import pallas as pl
from jax.experimental.pallas import tpu as pltpu
from jax.sharding import Mesh, PartitionSpec as P

SEQS = 4
PAIRS = 2
SLOTS = 40
LANES = 128
epsilon = 1e-05
dpo_beta = 0.5

AXES = ("x", "zl", "y", "zh", "c")
DP = ("x", "zl")
TENSOR = ("zh", "c")
OFFSETS = (0, 2, -1, 1)


f32 = jnp.float32
bf16 = jnp.bfloat16
VMEM = pl.BlockSpec(memory_space=pltpu.VMEM)
ANY = pl.BlockSpec(memory_space=pl.ANY)


def shift_pairs(sizes, dz=0, dc=0):
    nx, nl, ny, nh, nc = sizes
    nz = nh * nl

    def flat(x, y, z, c):
        return (((x * nl + z % nl) * ny + y) * nh + z // nl) * nc + c

    return [
        (flat(x, y, z, c), flat(x, y, (z + dz) % nz, (c + dc) % nc))
        for x in range(nx)
        for y in range(ny)
        for z in range(nz)
        for c in range(nc)
    ]


def exchange(array, axis):
    return lax.all_to_all(array, axis, 0, 0, tiled=True)


def for_each(array, count):
    return jnp.broadcast_to(array[None], (count, *array.shape))


def call(kernel, outs, ins, flops=0, in_specs=None, scratch=(), spare=4):
    size = sum(a.size * a.dtype.itemsize for a in (*ins, *outs))
    limit = min(size + (spare << 20), 60 << 20)
    return pl.pallas_call(
        kernel,
        out_shape=outs,
        in_specs=in_specs or [VMEM] * len(ins),
        out_specs=tuple(VMEM for _ in outs),
        scratch_shapes=list(scratch),
        compiler_params=pltpu.CompilerParams(vmem_limit_bytes=limit),
        cost_estimate=pl.CostEstimate(
            flops=flops or size, bytes_accessed=size, transcendentals=0
        ),
    )(*ins)


def column(row):
    return jnp.transpose(jnp.broadcast_to(row, (LANES, LANES)))


def front_kernel(own_count, columns, tok_ref, gain_ref, ids_ref, gw_ref, near_ref, far_ref, place_ref, gate_ref, res_ref):
    count, width = tok_ref.shape
    half = near_ref.shape[2]
    expert = lax.axis_index("y")
    core = lax.axis_index("c")
    step = 512
    squares = jnp.zeros((count, step), f32)
    for start in range(0, width, step):
        v = tok_ref[:, start : start + step].astype(f32)
        squares = squares + v * v
    total = jnp.sum(squares, axis=1, keepdims=True)
    inverse_rms = lax.rsqrt(total * (1.0 / width) + epsilon)
    match = ids_ref[...] == expert
    hit = match.astype(f32)
    named = hit[0:1] + hit[1:2]
    gate_row = jnp.sum(jnp.where(match, gw_ref[...], 0.0), axis=0, keepdims=True)
    gate_ref[...] = column(gate_row)
    before = lax.broadcasted_iota(jnp.int32, (count, count), 0)
    after = lax.broadcasted_iota(jnp.int32, (count, count), 1)
    position = jnp.dot(
        jnp.broadcast_to(named, (8, count)).astype(bf16),
        (before < after).astype(bf16),
        preferred_element_type=f32,
    )[0:1]
    slot = lax.broadcasted_iota(jnp.int32, (SLOTS, count), 0).astype(f32)
    place = jnp.where((slot == position) & (named > 0.5), 1.0, 0.0).astype(bf16)
    place_ref[...] = place
    nc = width // half
    column_at = (lax.axis_index("zh") * nc + core) * columns
    res_ref[...] = tok_ref[
        pl.ds(pl.multiple_of(expert * own_count, own_count), own_count),
        pl.ds(pl.multiple_of(column_at, LANES), columns),
    ]
    for start in range(0, half, step):
        at = pl.multiple_of(core * half + start, LANES)
        v = tok_ref[:, pl.ds(at, step)].astype(f32)
        normed = (v * inverse_rms * gain_ref[:, pl.ds(at, step)]).astype(bf16)
        rows = jnp.dot(place, normed, preferred_element_type=f32).astype(bf16)
        for x in range(near_ref.shape[0]):
            near_ref[x, :, start : start + step] = rows
        far_ref[:, start : start + step] = rows


def far_kernel(in_ref, out_ref):
    for x in range(out_ref.shape[0]):
        out_ref[x] = in_ref[...]


def slice_kernel(gate_ref, up_ref, send_ref, keep_ref, sems):
    half = send_ref.shape[1]
    core = lax.axis_index("c")
    copies = []
    for i, ref in enumerate((gate_ref, up_ref)):
        for j, (out, c) in enumerate(((send_ref, 1 - core), (keep_ref, core))):
            at = pl.multiple_of(c * half, 8)
            copies.append(
                pltpu.make_async_copy(
                    ref.at[0, pl.ds(at, half)], out.at[i], sems.at[2 * i + j]
                )
            )
    for copy in copies:
        copy.start()
    for copy in copies:
        copy.wait()


def dots_kernel(a_ref, b_ref, w_ref, *refs):
    *first, out_ref, sum_ref = refs
    _, half = a_ref.shape
    step = 512
    sum_ref[...] = jnp.zeros_like(sum_ref)

    def body(k, _):
        at = pl.multiple_of(k * step, step)
        x = jnp.concatenate(
            [a_ref[:, pl.ds(at, step)], b_ref[:, pl.ds(at, step)]], axis=0
        )
        w = jnp.concatenate(
            [w_ref[0, pl.ds(at, step), :], w_ref[1, pl.ds(at, step), :]], axis=1
        )
        sum_ref[...] += jnp.dot(x, w, preferred_element_type=f32)
        return 0

    lax.fori_loop(0, half // step, body, 0)
    at = 0
    for ref in first:
        out_ref[at : at + ref.shape[0]] = ref[...]
        at += ref.shape[0]
    out_ref[at:] = sum_ref[...]


def dots(a, b, w, *first):
    rows, half = a.shape
    wide = 2 * w.shape[2]
    out = jax.ShapeDtypeStruct((2 * rows + sum(p.shape[0] for p in first), wide), f32)
    (sums,) = call(
        dots_kernel,
        (out,),
        (a, b, w, *first),
        flops=2 * 2 * rows * half * wide,
        scratch=[pltpu.VMEM((2 * rows, wide), f32)],
    )
    return sums


def hidden_kernel(mine_ref, theirs_ref, out_ref):
    nx, nl, slots, units = out_ref.shape
    zl = lax.axis_index("zl")
    for r, offset in enumerate(OFFSETS):
        to = lax.rem(zl + offset + nl, nl)
        for x in range(nx):
            at = (r * nx + x) * slots
            sums = mine_ref[at : at + slots] + theirs_ref[at : at + slots]
            gate, up = sums[:, :units], sums[:, units:]
            out_ref[x, to] = (gate / (1.0 + jnp.exp(-gate)) * up).astype(bf16)


def stack_kernel(a_ref, b_ref, c_ref, out_ref):
    for i, ref in enumerate((a_ref, b_ref, c_ref)):
        out_ref[i] = ref[...]


def down_kernel(nh, mine_ref, other_ref, w_ref, out_ref):
    nx, rows, _ = out_ref.shape
    units = mine_ref.shape[2]
    zh = lax.axis_index("zh")
    core = lax.axis_index("c")
    weights = []
    for step in range(nh):
        base = lax.rem(zh + step, nh) * 2
        weights.append(
            jnp.concatenate(
                [
                    w_ref[0, pl.ds(pl.multiple_of((base + c) * units, units), units), :]
                    for c in (core, 1 - core)
                ],
                axis=0,
            )
        )
    for x in range(nx):
        part = pl.ds(x * rows, rows)
        total = 0.0
        for step in range(nh):
            block = jnp.concatenate(
                [mine_ref[step, part, :], other_ref[step, part, :]], axis=1
            )
            total = total + jnp.dot(block, weights[step], preferred_element_type=f32)
        out_ref[x] = total.astype(bf16)


def sum_kernel(in_ref, out_ref):
    total = in_ref[0].astype(f32)
    for i in range(1, in_ref.shape[0]):
        total = total + in_ref[i].astype(f32)
    out_ref[...] = total.astype(bf16).reshape(out_ref.shape)


def mix_kernel(in_ref, place_ref, gate_ref, labels_ref, seg_ref, res_ref, own_ref, out_ref, score_ref):
    ny, own_count, _ = out_ref.shape
    count, columns = labels_ref.shape
    expert = lax.axis_index("y")
    total = in_ref[0].astype(f32)
    for i in range(1, in_ref.shape[0]):
        total = total + in_ref[i].astype(f32)
    rows = total.astype(bf16)
    picked = lax.dot_general(
        place_ref[...], rows, (((0,), (0,)), ((), ())), preferred_element_type=f32
    )
    weighted = (gate_ref[:, 0:1] * picked).astype(bf16)
    row_score = jnp.sum(
        weighted.astype(f32) * labels_ref[...].astype(f32), axis=1, keepdims=True
    )
    score_ref[...] = jnp.broadcast_to(row_score, (count, LANES))
    own = jnp.sum(
        res_ref[...].astype(f32) * own_ref[...].astype(f32), axis=1, keepdims=True
    )
    at = pl.ds(pl.multiple_of(expert * own_count, own_count), own_count)
    score_ref[at, :] = score_ref[at, :] + jnp.broadcast_to(own, (own_count, LANES))
    sequence = column(seg_ref[...].astype(f32))
    lane = lax.broadcasted_iota(jnp.int32, (count, LANES), 1).astype(f32)
    member = jnp.where(sequence == lane, score_ref[...], 0.0)
    score = jnp.sum(member, axis=0, keepdims=True)
    first = score.astype(bf16).astype(f32)
    second = (score - first).astype(bf16).astype(f32)
    third = score - first - second
    row = lax.broadcasted_iota(jnp.int32, (own_count, LANES), 0)
    pads = jnp.where(
        row == 0,
        first,
        jnp.where(row == 1, second, jnp.where(row == 2, third, 0.0)),
    ).astype(bf16)
    for y in range(ny):
        out_ref[y, :, :columns] = weighted[y * own_count : (y + 1) * own_count]
        out_ref[y, :, columns:] = pads


def out_kernel(in_ref, res_ref, out_ref, score_ref):
    columns = out_ref.shape[1]
    total = in_ref[0].astype(f32)
    for y in range(1, in_ref.shape[0]):
        total = total + in_ref[y].astype(f32)
    out_ref[...] = (res_ref[...].astype(f32) + total[:, :columns]).astype(bf16)
    score = jnp.sum(total[:, columns:], axis=0, keepdims=True)
    for i in range(score_ref.shape[0]):
        score_ref[i] = score


def make_body(sizes):
    nx, nl, ny, nh, nc = sizes

    def shifted(array, dz=0, dc=0):
        return lax.ppermute(array, AXES, shift_pairs(sizes, dz, dc))

    def body(
        tokens,
        norm_gain,
        expert_ids,
        gate_weights,
        w_gate,
        w_up,
        w_down,
        label_rows,
        seg_ids,
        pair_slot,
        ref_scores,
    ):
        count, width = tokens.shape
        half = width // nc
        columns = width // (nh * nc)
        own_count = count // ny
        units = w_gate.shape[2]
        sds = jax.ShapeDtypeStruct
        own, own_far, place, gate, residual = call(
            functools.partial(front_kernel, own_count, columns),
            (
                sds((nx, SLOTS, half), bf16),
                sds((SLOTS, half), bf16),
                sds((SLOTS, count), bf16),
                sds((count, LANES), f32),
                sds((own_count, columns), bf16),
            ),
            (tokens, norm_gain[None, :], expert_ids.T, gate_weights.T),
            spare=60,
        )
        near = exchange(own, "x").reshape(nx * SLOTS, half)
        far = shifted(own_far, dz=2)
        w_send, w_mine = call(
            slice_kernel,
            (sds((2, half, units), bf16),) * 2,
            (w_gate, w_up),
            in_specs=[ANY, ANY],
            scratch=[pltpu.SemaphoreType.DMA((4,))],
            spare=60,
        )
        w_other = shifted(w_send, dc=1)
        below = shifted(near, dz=1)
        above = shifted(near, dz=-1)
        (far,) = call(far_kernel, (sds((nx, SLOTS, half), bf16),), (far,))
        far = exchange(far, "x").reshape(nx * SLOTS, half)
        early_other = dots(near, far, w_other)
        early_mine = dots(near, far, w_mine)
        below, above, early_mine = lax.optimization_barrier((below, above, early_mine))
        other = dots(below, above, w_other, early_other)
        theirs = shifted(other, dc=1)
        mine = dots(below, above, w_mine, early_mine)
        (hidden,) = call(
            hidden_kernel, (sds((nx, nl, SLOTS, units), bf16),), (mine, theirs)
        )
        hidden = hidden.reshape(nx * nl * SLOTS, units)
        labels = exchange(for_each(label_rows, ny), "y").reshape(count, columns)
        before = shifted(hidden, dz=nl)
        after = shifted(hidden, dz=-nl)
        (mine,) = call(
            stack_kernel, (sds((nh, *hidden.shape), bf16),), (hidden, after, before)
        )
        mine, labels = lax.optimization_barrier((mine, labels))
        others = shifted(mine, dc=1)
        (by_x,) = call(
            functools.partial(down_kernel, nh),
            (sds((nx, nl * SLOTS, columns), bf16),),
            (mine, others, w_down),
            flops=2 * hidden.shape[0] * w_down.shape[1] * columns,
        )
        by_x = exchange(by_x, "x")
        (by_zl,) = call(sum_kernel, (sds((nl, SLOTS, columns), bf16),), (by_x,))
        by_zl = exchange(by_zl, "zl")
        (sent,) = call(
            mix_kernel,
            (sds((ny, own_count, columns + LANES), bf16),),
            (by_zl, place, gate, labels, seg_ids, residual, label_rows),
            scratch=[pltpu.VMEM((count, LANES), f32)],
        )
        terms = exchange(sent, "y")
        layer_out, partial_value = call(
            out_kernel,
            (sds((own_count, columns), bf16), sds((nh * nc, 1, LANES), f32)),
            (terms, residual),
        )
        totals = exchange(partial_value, TENSOR)
        totals = jnp.sum(totals, axis=(0, 1))[:SEQS]
        slots_here = pair_slot[0]
        polarity = (1 - 2 * (slots_here % 2)).astype(f32)
        pair_member = (
            (slots_here // 2)[:, None]
            == jnp.arange(PAIRS, dtype=jnp.int32)[None, :]
        ).astype(f32)
        margins = dpo_beta * jnp.sum(
            pair_member * (polarity * (totals - ref_scores[0]))[:, None], axis=0
        )
        return (layer_out, margins[None, :])

    return body


def solution(mesh):
    sizes = (4, 4, mesh.shape["expert"], 3, 2)
    fine = Mesh(mesh.devices.reshape(sizes), AXES)
    placed = (
        P(DP, None),
        P(),
        P(DP, None),
        P(DP, None),
        P("y", None, (*DP, *TENSOR)),
        P("y", None, (*DP, *TENSOR)),
        P("y", DP, TENSOR),
        P((*DP, "y"), TENSOR),
        P(DP, None),
        P(DP, None),
        P(DP, None),
    )
    return jax.shard_map(
        make_body(sizes),
        mesh=fine,
        in_specs=placed,
        out_specs=(P((*DP, "y"), TENSOR), P(DP, None)),
        check_vma=False,
    )
```

profile of v0, /device:TPU:1, one launch (start us, length us, event | category | flops | bytes accessed | tf_op | source)
XLA Modules:
  0.0 181.3 jit_solution(5053943593134175717)
XLA Ops:
  0.6 3.1 %shard_map.122 = (bf16[4,40,3072]{2,1,0:T(8,128)(2,1)}, bf16[40,3072]{1,0:T(8,128)(2,1)}, bf16[40,128]{1,0:T(8,128)(2,1)}, f32[128,128]{1,0:T(8,128)}, bf16[16,1024]{1,0:T(8,128)(2,1)}) custom-call(bf16[128,6144]{1,0:T(8,128)(2,1)} %tok_ref.1, f32[1,6144]{1,0:T(1,128)} %bitcast.37, s32[2,128]{1,0:T(2,128)} %bitcast.38, f32[2,128]{1,0:T(2,128)} %bitcast.39), custom_call_target="tpu_custom_call" | custom-call | flops 2936832 | bytes 2936832 | tf_op jit(solution)/shard_map/pallas_call | solution.py:56
  3.7 4.8 %all-to-all-start = ((bf16[4,40,3072]{2,1,0:T(8,128)(2,1)}), bf16[4,40,3072]{2,1,0:T(8,128)(2,1)S(1)}, u32[]{:S(2)}, u32[]{:S(2)}) async-start(bf16[4,40,3072]{2,1,0:T(8,128)(2,1)} %get-tuple-element.16), calls=%async_computation | async-start | bytes 1966080 | tf_op jit(solution)/shard_map/all_to_all | solution.py:46
  8.6 3.6 %shard_map.124 = (bf16[2,3072,128]{2,1,0:T(8,128)(2,1)}, bf16[2,3072,128]{2,1,0:T(8,128)(2,1)}) custom-call(bf16[1,6144,128]{2,1,0:T(8,128)(2,1)} %gate_ref.1, bf16[1,6144,128]{2,1,0:T(8,128)(2,1)} %up_ref.1), custom_call_target="tpu_custom_call" | custom-call | flops 6291456 | bytes 6291456 | tf_op jit(solution)/shard_map/pallas_call | solution.py:56
  12.1 11.1 %collective-permute-start.3 = (bf16[2,3072,128]{2,1,0:T(8,128)(2,1)}, bf16[2,3072,128]{2,1,0:T(8,128)(2,1)}, u32[]{:S(2)}, u32[]{:S(2)}) collective-permute-start(bf16[2,3072,128]{2,1,0:T(8,128)(2,1)} %get-tuple-element.22), channel_id=1, source_target_pairs={{0,1},{1,0},{48,49},{49,48},{96,97},{97,96},{144,145},{145,144},{2... | collective-permute-start | bytes 4718600 | tf_op jit(solution)/shard_map/ppermute | solution.py:284
  23.2 1.9 %collective-permute-start.2 = (bf16[40,3072]{1,0:T(8,128)(2,1)}, bf16[40,3072]{1,0:T(8,128)(2,1)}, u32[]{:S(2)}, u32[]{:S(2)}) collective-permute-start(bf16[40,3072]{1,0:T(8,128)(2,1)} %get-tuple-element.17), channel_id=1, source_target_pairs={{0,96},{1,97},{48,144},{49,145},{96,2},{97,3},{144,50},{145,51},{2... | collective-permute-start | bytes 737288 | tf_op jit(solution)/shard_map/ppermute | solution.py:284
  25.2 2.1 %collective-permute-start = (bf16[160,3072]{1,0:T(8,128)(2,1)S(1)}, bf16[160,3072]{1,0:T(8,128)(2,1)S(1)}, u32[]{:S(2)}, u32[]{:S(2)}) collective-permute-start(bf16[160,3072]{1,0:T(8,128)(2,1)S(1)} %bitcast.28), channel_id=1, source_target_pairs={{0,48},{1,49},{48,96},{49,97},{96,144},{97,145},{144,2},{145,3},{2... | collective-permute-start | bytes 2949128 | tf_op jit(solution)/shard_map/ppermute | solution.py:284
  27.2 11.2 %collective-permute-start.1 = (bf16[160,3072]{1,0:T(8,128)(2,1)S(1)}, bf16[160,3072]{1,0:T(8,128)(2,1)S(1)}, u32[]{:S(2)}, u32[]{:S(2)}) collective-permute-start(bf16[160,3072]{1,0:T(8,128)(2,1)S(1)} %bitcast.29), channel_id=1, source_target_pairs={{0,148},{1,149},{48,0},{49,1},{96,48},{97,49},{144,96},{145,97},{2... | collective-permute-start | bytes 2949128 | tf_op jit(solution)/shard_map/ppermute | solution.py:284
  38.5 1.0 shard_map.123
  39.5 15.0 %all_to_all.35 = bf16[4,40,3072]{2,1,0:T(8,128)(2,1)S(1)} all-to-all(bf16[4,40,3072]{2,1,0:T(8,128)(2,1)S(1)} %shard_map.123), channel_id=1, replica_groups=mesh['x'=4,'zl'=4,'y'=8,'zh'=3,'c'=2] {'x'}, dimensions={0} | all-to-all | bytes 1966080 | tf_op jit(solution)/shard_map/all_to_all | solution.py:46
  54.5 1.5 shard_map.125.refs_0_
  56.0 3.0 %shard_map.127.refs_0_ = f32[320,256]{1,0:T(8,128)S(1)} custom-call(bf16[160,3072]{1,0:T(8,128)(2,1)S(1)} %bitcast.31, bf16[160,3072]{1,0:T(8,128)(2,1)S(1)} %bitcast.33, bf16[2,3072,128]{2,1,0:T(8,128)(2,1)} %collective-permute-done.3.w_ref), custom_call_target="tpu_custom_call" | custom-call | flops 503316480 | bytes 3866624 | tf_op jit(solution)/shard_map/pallas_call | solution.py:56
  59.1 3.3 %collective-permute-done.a_ref = bf16[160,3072]{1,0:T(8,128)(2,1)S(1)} collective-permute-done((bf16[160,3072]{1,0:T(8,128)(2,1)S(1)}, bf16[160,3072]{1,0:T(8,128)(2,1)S(1)}, u32[]{:S(2)}, u32[]{:S(2)}) %collective-permute-start) | collective-permute-done | bytes 983072 | tf_op jit(solution)/shard_map/ppermute | solution.py:284
  62.4 4.2 %shard_map.128 = f32[640,256]{1,0:T(8,128)} custom-call(bf16[160,3072]{1,0:T(8,128)(2,1)S(1)} %collective-permute-done.a_ref, bf16[160,3072]{1,0:T(8,128)(2,1)S(1)} %collective-permute-done.1.b_ref, bf16[2,3072,128]{2,1,0:T(8,128)(2,1)} %collective-permute-done.3.w_ref, f32[320,256]{1,0:T(8,128)S(1)} %shard_map.127.refs_0_), custom_call_target="tpu_custom_call" | custom-call | flops 503316480 | bytes 4521984 | tf_op jit(solution)/shard_map/pallas_call | solution.py:56
  66.6 2.3 %collective-permute-start.4 = (f32[640,256]{1,0:T(8,128)}, f32[640,256]{1,0:T(8,128)}, u32[]{:S(2)}, u32[]{:S(2)}) collective-permute-start(f32[640,256]{1,0:T(8,128)} %shard_map.128), channel_id=1, source_target_pairs={{0,1},{1,0},{48,49},{49,48},{96,97},{97,96},{144,145},{145,144},{2... | collective-permute-start | bytes 1966088 | tf_op jit(solution)/shard_map/ppermute | solution.py:284
  68.9 0.7 broadcast_in_dim.5
  69.6 10.6 %all-to-all-start.2 = ((bf16[8,16,1024]{2,1,0:T(8,128)(2,1)}), bf16[8,16,1024]{2,1,0:T(8,128)(2,1)}, u32[]{:S(2)}, u32[]{:S(2)}) async-start(bf16[8,16,1024]{2,1,0:T(8,128)(2,1)} %broadcast_in_dim.5), calls=%async_computation.2 | async-start | bytes 524288 | tf_op jit(solution)/shard_map/all_to_all | solution.py:46
  80.2 1.2 copy-done.2
  81.4 1.5 shard_map.126.mine_ref
  83.0 1.3 shard_map.129
  84.3 5.2 %collective-permute-start.5 = (bf16[640,128]{1,0:T(8,128)(2,1)S(1)}, bf16[640,128]{1,0:T(8,128)(2,1)S(1)}, u32[]{:S(2)}, u32[]{:S(2)}) collective-permute-start(bf16[640,128]{1,0:T(8,128)(2,1)S(1)} %bitcast.34), channel_id=1, source_target_pairs={{0,4},{1,5},{48,52},{49,53},{96,100},{97,101},{144,148},{145,149},... | collective-permute-start | bytes 491528 | tf_op jit(solution)/shard_map/ppermute | solution.py:284
  89.5 4.0 %collective-permute-start.6 = (bf16[640,128]{1,0:T(8,128)(2,1)S(1)}, bf16[640,128]{1,0:T(8,128)(2,1)S(1)}, u32[]{:S(2)}, u32[]{:S(2)}) collective-permute-start(bf16[640,128]{1,0:T(8,128)(2,1)S(1)} %bitcast.35), channel_id=1, source_target_pairs={{0,2},{1,3},{48,50},{49,51},{96,98},{97,99},{144,146},{145,147},{2... | collective-permute-start | bytes 491528 | tf_op jit(solution)/shard_map/ppermute | solution.py:284
  93.5 9.5 %collective-permute-done.5.b_ref = bf16[640,128]{1,0:T(8,128)(2,1)S(1)} collective-permute-done((bf16[640,128]{1,0:T(8,128)(2,1)S(1)}, bf16[640,128]{1,0:T(8,128)(2,1)S(1)}, u32[]{:S(2)}, u32[]{:S(2)}) %collective-permute-start.5) | collective-permute-done | bytes 163872 | tf_op jit(solution)/shard_map/ppermute | solution.py:284
  103.0 1.4 collective-permute-done.6.c_ref
  104.5 2.8 %collective-permute-start.7 = (bf16[3,640,128]{2,1,0:T(8,128)(2,1)S(1)}, bf16[3,640,128]{2,1,0:T(8,128)(2,1)S(1)}, u32[]{:S(2)}, u32[]{:S(2)}) collective-permute-start(bf16[3,640,128]{2,1,0:T(8,128)(2,1)S(1)} %shard_map.130.mine_ref), channel_id=1, source_target_pairs={{0,1},{1,0},{48,49},{49,48},{96,97},{97,96},{144,145},{145,144},{2... | collective-permute-start | bytes 1474568 | tf_op jit(solution)/shard_map/ppermute | solution.py:284
  107.3 1.5 collective-permute-done.7.other_ref
  108.8 1.2 shard_map.131
  110.0 22.9 %all_to_all.36.in_ref = bf16[4,160,1024]{2,1,0:T(8,128)(2,1)S(1)} all-to-all(bf16[4,160,1024]{2,1,0:T(8,128)(2,1)S(1)} %shard_map.131), channel_id=1, replica_groups=mesh['x'=4,'zl'=4,'y'=8,'zh'=3,'c'=2] {'x'}, dimensions={0} | all-to-all | bytes 2621440 | tf_op jit(solution)/shard_map/all_to_all | solution.py:46
  133.1 10.7 %all_to_all.37.in_ref = bf16[4,40,1024]{2,1,0:T(8,128)(2,1)S(1)} all-to-all(bf16[4,40,1024]{2,1,0:T(8,128)(2,1)S(1)} %shard_map.132), channel_id=1, replica_groups=mesh['x'=4,'zl'=4,'y'=8,'zh'=3,'c'=2] {'zl'}, dimensions={0} | all-to-all | bytes 655360 | tf_op jit(solution)/shard_map/all_to_all | solution.py:46
  143.9 1.4 shard_map.133
  145.2 16.1 %all_to_all.38.in_ref = bf16[8,16,1152]{2,1,0:T(8,128)(2,1)S(1)} all-to-all(bf16[8,16,1152]{2,1,0:T(8,128)(2,1)S(1)} %shard_map.133), channel_id=1, replica_groups=mesh['x'=4,'zl'=4,'y'=8,'zh'=3,'c'=2] {'y'}, dimensions={0} | all-to-all | bytes 589824 | tf_op jit(solution)/shard_map/all_to_all | solution.py:46
  162.0 11.6 %all-to-all-start.6 = ((f32[6,1,128]{2,1,0:T(1,128)}), f32[6,1,128]{2,1,0:T(1,128)S(1)}, u32[]{:S(2)}, u32[]{:S(2)}) async-start(f32[6,1,128]{2,1,0:T(1,128)} %get-tuple-element.29), calls=%async_computation.6 | async-start | bytes 6144 | tf_op jit(solution)/shard_map/all_to_all | solution.py:46
  173.6 7.0 %all-to-all-done.6 = f32[6,1,128]{2,1,0:T(1,128)S(1)} async-done(((f32[6,1,128]{2,1,0:T(1,128)}), f32[6,1,128]{2,1,0:T(1,128)S(1)}, u32[]{:S(2)}, u32[]{:S(2)}) %all-to-all-start.6) | async-done | bytes 3104 | tf_op jit(solution)/shard_map/all_to_all | solution.py:46
  (41 shorter events, 1.6 us)
Async XLA Ops:
  3.7 21.4 %all-to-all-start = ((bf16[4,40,3072]{2,1,0:T(8,128)(2,1)}), bf16[4,40,3072]{2,1,0:T(8,128)(2,1)S(1)}, u32[]{:S(2)}, u32[]{:S(2)}) async-start(bf16[4,40,3072]{2,1,0:T(8,128)(2,1)} %get-tuple-element.16), calls=%async_computation | async-start | bytes 1966080 | tf_op jit(solution)/shard_map/all_to_all | solution.py:46
  12.1 43.9 %collective-permute-start.3 = (bf16[2,3072,128]{2,1,0:T(8,128)(2,1)}, bf16[2,3072,128]{2,1,0:T(8,128)(2,1)}, u32[]{:S(2)}, u32[]{:S(2)}) collective-permute-start(bf16[2,3072,128]{2,1,0:T(8,128)(2,1)} %get-tuple-element.22), channel_id=1, source_target_pairs={{0,1},{1,0},{48,49},{49,48},{96,97},{97,96},{144,145},{145,144},{2... | collective-permute-start | bytes 4718600 | tf_op jit(solution)/shard_map/ppermute | solution.py:284
  23.2 15.3 %collective-permute-start.2 = (bf16[40,3072]{1,0:T(8,128)(2,1)}, bf16[40,3072]{1,0:T(8,128)(2,1)}, u32[]{:S(2)}, u32[]{:S(2)}) collective-permute-start(bf16[40,3072]{1,0:T(8,128)(2,1)} %get-tuple-element.17), channel_id=1, source_target_pairs={{0,96},{1,97},{48,144},{49,145},{96,2},{97,3},{144,50},{145,51},{2... | collective-permute-start | bytes 737288 | tf_op jit(solution)/shard_map/ppermute | solution.py:284
  25.2 29.3 %copy-start = (bf16[2,3072,128]{2,1,0:T(8,128)(2,1)S(1)}, bf16[2,3072,128]{2,1,0:T(8,128)(2,1)}, u32[]{:S(2)}) copy-start(bf16[2,3072,128]{2,1,0:T(8,128)(2,1)} %get-tuple-element.18.w_ref) | copy-start | bytes 4718596
  25.2 37.2 %collective-permute-start = (bf16[160,3072]{1,0:T(8,128)(2,1)S(1)}, bf16[160,3072]{1,0:T(8,128)(2,1)S(1)}, u32[]{:S(2)}, u32[]{:S(2)}) collective-permute-start(bf16[160,3072]{1,0:T(8,128)(2,1)S(1)} %bitcast.28), channel_id=1, source_target_pairs={{0,48},{1,49},{48,96},{49,97},{96,144},{97,145},{144,2},{145,3},{2... | collective-permute-start | bytes 2949128 | tf_op jit(solution)/shard_map/ppermute | solution.py:284
  27.2 35.2 %collective-permute-start.1 = (bf16[160,3072]{1,0:T(8,128)(2,1)S(1)}, bf16[160,3072]{1,0:T(8,128)(2,1)S(1)}, u32[]{:S(2)}, u32[]{:S(2)}) collective-permute-start(bf16[160,3072]{1,0:T(8,128)(2,1)S(1)} %bitcast.29), channel_id=1, source_target_pairs={{0,148},{1,149},{48,0},{49,1},{96,48},{97,49},{144,96},{145,97},{2... | collective-permute-start | bytes 2949128 | tf_op jit(solution)/shard_map/ppermute | solution.py:284
  56.0 3.1 %copy-start.4 = (f32[320,256]{1,0:T(8,128)}, f32[320,256]{1,0:T(8,128)S(1)}, u32[]{:S(2)}) copy-start(f32[320,256]{1,0:T(8,128)S(1)} %shard_map.125.refs_0_) | copy-start | bytes 983044
  59.1 9.8 %copy-start.6 = (bf16[16,1024]{1,0:T(8,128)(2,1)S(1)}, bf16[16,1024]{1,0:T(8,128)(2,1)}, u32[]{:S(2)}) copy-start(bf16[16,1024]{1,0:T(8,128)(2,1)} %own_ref.1) | copy-start | bytes 98308
  62.4 4.2 %copy-start.1 = (bf16[160,3072]{1,0:T(8,128)(2,1)}, bf16[160,3072]{1,0:T(8,128)(2,1)S(1)}, u32[]{:S(2)}) copy-start(bf16[160,3072]{1,0:T(8,128)(2,1)S(1)} %collective-permute-done.1.b_ref) | copy-start | bytes 2949124
  62.4 17.8 %copy-start.5 = (f32[320,256]{1,0:T(8,128)S(1)}, f32[320,256]{1,0:T(8,128)}, u32[]{:S(2)}) copy-start(f32[320,256]{1,0:T(8,128)} %copy-done.4) | copy-start | bytes 983044
  66.6 16.4 %collective-permute-start.4 = (f32[640,256]{1,0:T(8,128)}, f32[640,256]{1,0:T(8,128)}, u32[]{:S(2)}, u32[]{:S(2)}) collective-permute-start(f32[640,256]{1,0:T(8,128)} %shard_map.128), channel_id=1, source_target_pairs={{0,1},{1,0},{48,49},{49,48},{96,97},{97,96},{144,145},{145,144},{2... | collective-permute-start | bytes 1966088 | tf_op jit(solution)/shard_map/ppermute | solution.py:284
  69.6 34.9 %all-to-all-start.2 = ((bf16[8,16,1024]{2,1,0:T(8,128)(2,1)}), bf16[8,16,1024]{2,1,0:T(8,128)(2,1)}, u32[]{:S(2)}, u32[]{:S(2)}) async-start(bf16[8,16,1024]{2,1,0:T(8,128)(2,1)} %broadcast_in_dim.5), calls=%async_computation.2 | async-start | bytes 524288 | tf_op jit(solution)/shard_map/all_to_all | solution.py:46
  80.2 1.2 copy-start.2
  83.0 25.9 %copy-start.3 = (bf16[1,768,1024]{2,1,0:T(8,128)(2,1)S(1)}, bf16[1,768,1024]{2,1,0:T(8,128)(2,1)}, u32[]{:S(2)}) copy-start(bf16[1,768,1024]{2,1,0:T(8,128)(2,1)} %w_ref.1) | copy-start | bytes 4718596
  84.3 18.7 %collective-permute-start.5 = (bf16[640,128]{1,0:T(8,128)(2,1)S(1)}, bf16[640,128]{1,0:T(8,128)(2,1)S(1)}, u32[]{:S(2)}, u32[]{:S(2)}) collective-permute-start(bf16[640,128]{1,0:T(8,128)(2,1)S(1)} %bitcast.34), channel_id=1, source_target_pairs={{0,4},{1,5},{48,52},{49,53},{96,100},{97,101},{144,148},{145,149},... | collective-permute-start | bytes 491528 | tf_op jit(solution)/shard_map/ppermute | solution.py:284
  89.5 14.9 %collective-permute-start.6 = (bf16[640,128]{1,0:T(8,128)(2,1)S(1)}, bf16[640,128]{1,0:T(8,128)(2,1)S(1)}, u32[]{:S(2)}, u32[]{:S(2)}) collective-permute-start(bf16[640,128]{1,0:T(8,128)(2,1)S(1)} %bitcast.35), channel_id=1, source_target_pairs={{0,2},{1,3},{48,50},{49,51},{96,98},{97,99},{144,146},{145,147},{2... | collective-permute-start | bytes 491528 | tf_op jit(solution)/shard_map/ppermute | solution.py:284
  104.5 4.3 %collective-permute-start.7 = (bf16[3,640,128]{2,1,0:T(8,128)(2,1)S(1)}, bf16[3,640,128]{2,1,0:T(8,128)(2,1)S(1)}, u32[]{:S(2)}, u32[]{:S(2)}) collective-permute-start(bf16[3,640,128]{2,1,0:T(8,128)(2,1)S(1)} %shard_map.130.mine_ref), channel_id=1, source_target_pairs={{0,1},{1,0},{48,49},{49,48},{96,97},{97,96},{144,145},{145,144},{2... | collective-permute-start | bytes 1474568 | tf_op jit(solution)/shard_map/ppermute | solution.py:284
  132.9 10.9 %copy-start.7 = (bf16[16,1024]{1,0:T(8,128)(2,1)S(1)}, bf16[16,1024]{1,0:T(8,128)(2,1)}, u32[]{:S(2)}) copy-start(bf16[16,1024]{1,0:T(8,128)(2,1)} %own_ref.1) | copy-start | bytes 98308
  132.9 10.9 %copy-start.8 = (bf16[16,1024]{1,0:T(8,128)(2,1)S(1)}, bf16[16,1024]{1,0:T(8,128)(2,1)}, u32[]{:S(2)}) copy-start(bf16[16,1024]{1,0:T(8,128)(2,1)} %get-tuple-element.27.res_ref) | copy-start | bytes 98308
  132.9 10.9 %copy-start.9 = (f32[128,128]{1,0:T(8,128)S(1)}, f32[128,128]{1,0:T(8,128)}, u32[]{:S(2)}) copy-start(f32[128,128]{1,0:T(8,128)} %get-tuple-element.25.gate_ref) | copy-start | bytes 196612
  132.9 10.9 %copy-start.10 = (bf16[40,128]{1,0:T(8,128)(2,1)S(1)}, bf16[40,128]{1,0:T(8,128)(2,1)}, u32[]{:S(2)}) copy-start(bf16[40,128]{1,0:T(8,128)(2,1)} %get-tuple-element.24.place_ref) | copy-start | bytes 30724
  132.9 10.9 %copy-start.11 = (s32[1,128]{1,0:T(1,128)S(1)}, s32[1,128]{1,0:T(1,128)}, u32[]{:S(2)}) copy-start(s32[1,128]{1,0:T(1,128)} %seg_ref.1) | copy-start | bytes 1540
  133.1 40.5 %copy-start.13 = (s32[1,4]{1,0:T(1,128)S(1)}, s32[1,4]{1,0:T(1,128)}, u32[]{:S(2)}) copy-start(s32[1,4]{1,0:T(1,128)} %param.20) | copy-start | bytes 52
  133.1 47.5 %copy-start.12 = (f32[1,4]{1,0:T(1,128)S(1)}, f32[1,4]{1,0:T(1,128)}, u32[]{:S(2)}) copy-start(f32[1,4]{1,0:T(1,128)} %param.21) | copy-start | bytes 52
  162.0 18.6 %all-to-all-start.6 = ((f32[6,1,128]{2,1,0:T(1,128)}), f32[6,1,128]{2,1,0:T(1,128)S(1)}, u32[]{:S(2)}, u32[]{:S(2)}) async-start(f32[6,1,128]{2,1,0:T(1,128)} %get-tuple-element.29), calls=%async_computation.6 | async-start | bytes 6144 | tf_op jit(solution)/shard_map/all_to_all | solution.py:46
where the time goes:
time: 182 us; the launch traced here: 181 us
  starting transfers between devices  67.6 us (37%)
  blocking collectives  64.7 us (36%)
  Pallas kernels  22.7 us (12%)
  waiting for transfers between devices  22.7 us (12%)
  local copies, waits for them, and re-layouts  2 us (1%)
    all_to_all x4, blocking collectives, exchange(): return lax.all_to_all(array, axis, 0, 0, tiled=True)  64.7 us
    ppermute x8, starting transfers between devices, shifted(): return lax.ppermute(array, AXES, shift_pairs(sizes, dz, dc))  40.6 us
    all_to_all x3, starting transfers between devices, exchange(): return lax.all_to_all(array, axis, 0, 0, tiled=True)  26.9 us
    pallas_call x13, Pallas kernels, call(): pl.pallas_call(kernel, out_shape=outs, in_specs=in_specs or [VMEM] * len(...  22.7 us
    ppermute x8, waiting for transfers between devices, shifted(): return lax.ppermute(array, AXES, shift_pairs(sizes, dz, dc))  15.7 us
    all_to_all x3, waiting for transfers between devices, exchange(): return lax.all_to_all(array, axis, 0, 0, tiled=True)  6.99 us
  transfers between devices with their start and end apart: 11, of which 5 were waited for; matrix products, arithmetic and copies ran while one was open for 0% of the time, Pallas kernels for 7%

commit v1 on v0

--- a/solution.py
+++ b/solution.py
@@ -9,7 +9,7 @@
 
 SEQS = 4
 PAIRS = 2
-SLOTS = 40
+SLOTS = 36
 LANES = 128
 epsilon = 1e-05
 dpo_beta = 0.5
@@ -23,10 +23,10 @@
 f32 = jnp.float32
 bf16 = jnp.bfloat16
 VMEM = pl.BlockSpec(memory_space=pltpu.VMEM)
-ANY = pl.BlockSpec(memory_space=pl.ANY)
-
-
-def shift_pairs(sizes, dz=0, dc=0):
+HBM = pl.BlockSpec(memory_space=pltpu.HBM)
+
+
+def shift_pairs(sizes, dx=0, dy=0, dz=0, dc=0):
     nx, nl, ny, nh, nc = sizes
     nz = nh * nl
 
@@ -34,7 +34,10 @@
         return (((x * nl + z % nl) * ny + y) * nh + z // nl) * nc + c
 
     return [
-        (flat(x, y, z, c), flat(x, y, (z + dz) % nz, (c + dc) % nc))
+        (
+            flat(x, y, z, c),
+            flat((x + dx) % nx, (y + dy) % ny, (z + dz) % nz, (c + dc) % nc),
+        )
         for x in range(nx)
         for y in range(ny)
         for z in range(nz)
@@ -44,10 +47,6 @@
 
 def exchange(array, axis):
     return lax.all_to_all(array, axis, 0, 0, tiled=True)
-
-
-def for_each(array, count):
-    return jnp.broadcast_to(array[None], (count, *array.shape))
 
 
 def call(kernel, outs, ins, flops=0, in_specs=None, scratch=(), spare=4):
@@ -70,9 +69,19 @@
     return jnp.transpose(jnp.broadcast_to(row, (LANES, LANES)))
 
 
-def front_kernel(own_count, columns, tok_ref, gain_ref, ids_ref, gw_ref, near_ref, far_ref, place_ref, gate_ref, res_ref):
+def front_kernel(own_count, columns, *refs):
+    *ins, own_ref, far_ref, place_ref, gate_ref, res_ref, tok_ref, gain_ref, ids_ref, gw_ref, sems = refs
+    copies = [
+        pltpu.make_async_copy(ref, held, sems.at[i])
+        for i, (ref, held) in enumerate(
+            zip(ins, (tok_ref, gain_ref, ids_ref, gw_ref), strict=True)
+        )
+    ]
+    for copy in copies:
+        copy.start()
+    for copy in copies:
+        copy.wait()
     count, width = tok_ref.shape
-    half = near_ref.shape[2]
     expert = lax.axis_index("y")
     core = lax.axis_index("c")
     step = 512
@@ -94,28 +103,58 @@
         (before < after).astype(bf16),
         preferred_element_type=f32,
     )[0:1]
-    slot = lax.broadcasted_iota(jnp.int32, (SLOTS, count), 0).astype(f32)
-    place = jnp.where((slot == position) & (named > 0.5), 1.0, 0.0).astype(bf16)
-    place_ref[...] = place
+    slot = lax.broadcasted_iota(jnp.int32, (2 * SLOTS, count), 0).astype(f32)
+    here = named > 0.5
+    upper = jnp.where((slot == position) & here, 1.0, 0.0).astype(bf16)
+    lower = jnp.where((slot - SLOTS == position) & here, 1.0, 0.0).astype(bf16)
+    place_ref[...] = upper
+    fold = own_ref.shape[2]
+    half = 2 * fold
     nc = width // half
     column_at = (lax.axis_index("zh") * nc + core) * columns
     res_ref[...] = tok_ref[
         pl.ds(pl.multiple_of(expert * own_count, own_count), own_count),
         pl.ds(pl.multiple_of(column_at, LANES), columns),
     ]
-    for start in range(0, half, step):
+
+    def normed(start):
         at = pl.multiple_of(core * half + start, LANES)
         v = tok_ref[:, pl.ds(at, step)].astype(f32)
-        normed = (v * inverse_rms * gain_ref[:, pl.ds(at, step)]).astype(bf16)
-        rows = jnp.dot(place, normed, preferred_element_type=f32).astype(bf16)
-        for x in range(near_ref.shape[0]):
-            near_ref[x, :, start : start + step] = rows
+        return (v * inverse_rms * gain_ref[:, pl.ds(at, step)]).astype(bf16)
+
+    for start in range(0, fold, step):
+        rows = jnp.dot(upper, normed(start), preferred_element_type=f32)
+        rows += jnp.dot(lower, normed(start + fold), preferred_element_type=f32)
+        rows = rows.astype(bf16)
+        for x in range(own_ref.shape[0]):
+            own_ref[x, :, start : start + step] = rows
         far_ref[:, start : start + step] = rows
 
 
-def far_kernel(in_ref, out_ref):
+def copies_kernel(in_ref, out_ref):
     for x in range(out_ref.shape[0]):
         out_ref[x] = in_ref[...]
+
+
+def pack_kernel(in_ref, out_ref):
+    blocks, folded, fold = in_ref.shape
+    rows = out_ref.shape[0]
+    step = 512
+    to = lax.broadcasted_iota(jnp.int32, (rows, blocks * folded), 0)
+    source = lax.broadcasted_iota(jnp.int32, (rows, blocks * folded), 1)
+    for side in range(2):
+        at = jnp.where(source < 0, 0, -1)
+        for x in range(blocks):
+            base = x * folded + side * SLOTS
+            inside = (source >= base) & (source < base + SLOTS)
+            at = jnp.where(inside, source - base + x * SLOTS, at)
+        chosen = jnp.where(at == to, 1.0, 0.0).astype(bf16)
+        for start in range(0, fold, step):
+            block = jnp.concatenate(
+                [in_ref[x, :, start : start + step] for x in range(blocks)], axis=0
+            )
+            moved = jnp.dot(chosen, block, preferred_element_type=f32).astype(bf16)
+            out_ref[:, side * fold + start : side * fold + start + step] = moved
 
 
 def slice_kernel(gate_ref, up_ref, send_ref, keep_ref, sems):
@@ -175,31 +214,37 @@
     return sums
 
 
-def hidden_kernel(mine_ref, theirs_ref, out_ref):
-    nx, nl, slots, units = out_ref.shape
-    zl = lax.axis_index("zl")
-    for r, offset in enumerate(OFFSETS):
-        to = lax.rem(zl + offset + nl, nl)
-        for x in range(nx):
-            at = (r * nx + x) * slots
-            sums = mine_ref[at : at + slots] + theirs_ref[at : at + slots]
-            gate, up = sums[:, :units], sums[:, units:]
-            out_ref[x, to] = (gate / (1.0 + jnp.exp(-gate)) * up).astype(bf16)
-
-
-def stack_kernel(a_ref, b_ref, c_ref, out_ref):
-    for i, ref in enumerate((a_ref, b_ref, c_ref)):
-        out_ref[i] = ref[...]
-
-
-def down_kernel(nh, mine_ref, other_ref, w_ref, out_ref):
+def hidden_kernel(nx, mine_ref, theirs_ref, out_ref):
+    _, total, units = out_ref.shape
+    block = total // nx
+    parts = []
+    for start in range(0, total, block):
+        sums = mine_ref[start : start + block] + theirs_ref[start : start + block]
+        gate, up = sums[:, :units], sums[:, units:]
+        parts.append((gate / (1.0 + jnp.exp(-gate)) * up).astype(bf16))
+    hidden = jnp.concatenate(parts, axis=0)
+    slot = lax.broadcasted_iota(jnp.int32, (block, total), 0)
+    source = lax.broadcasted_iota(jnp.int32, (block, total), 1)
+    for x in range(nx):
+        at = jnp.where(source < 0, 0, -1)
+        for r in range(total // block):
+            base = r * block + x * SLOTS
+            inside = (source >= base) & (source < base + SLOTS)
+            at = jnp.where(inside, source - base + r * SLOTS, at)
+        chosen = jnp.where(at == slot, 1.0, 0.0).astype(bf16)
+        moved = jnp.dot(chosen, hidden, preferred_element_type=f32)
+        moved = moved.astype(bf16)
+        for i in range(out_ref.shape[0]):
+            out_ref[i, x * block : (x + 1) * block] = moved
+
+
+def down_kernel(mine_ref, other_ref, w_ref, out_ref):
     nx, rows, _ = out_ref.shape
-    units = mine_ref.shape[2]
-    zh = lax.axis_index("zh")
+    nh, _, units = mine_ref.shape
     core = lax.axis_index("c")
     weights = []
     for step in range(nh):
-        base = lax.rem(zh + step, nh) * 2
+        base = step * 2
         weights.append(
             jnp.concatenate(
                 [
@@ -221,28 +266,52 @@
 
 
 def sum_kernel(in_ref, out_ref):
+    nl, slots, _ = out_ref.shape
+    rows = in_ref.shape[1]
+    zl = lax.axis_index("zl")
     total = in_ref[0].astype(f32)
     for i in range(1, in_ref.shape[0]):
         total = total + in_ref[i].astype(f32)
-    out_ref[...] = total.astype(bf16).reshape(out_ref.shape)
+    total = total.astype(bf16)
+    slot = lax.broadcasted_iota(jnp.int32, (slots, rows), 0)
+    source = lax.broadcasted_iota(jnp.int32, (slots, rows), 1)
+    for r, offset in enumerate(OFFSETS):
+        chosen = jnp.where(source == slot + r * SLOTS, 1.0, 0.0).astype(bf16)
+        moved = jnp.dot(chosen, total, preferred_element_type=f32)
+        out_ref[lax.rem(zl + offset + nl, nl)] = moved.astype(bf16)
+
+
+def join_kernel(a_ref, b_ref, out_ref):
+    size = a_ref.shape[0]
+    out_ref[:size] = a_ref[...]
+    out_ref[size:] = b_ref[...]
 
 
 def mix_kernel(in_ref, place_ref, gate_ref, labels_ref, seg_ref, res_ref, own_ref, out_ref, score_ref):
     ny, own_count, _ = out_ref.shape
-    count, columns = labels_ref.shape
+    count, columns = ny * own_count, labels_ref.shape[2]
     expert = lax.axis_index("y")
     total = in_ref[0].astype(f32)
     for i in range(1, in_ref.shape[0]):
         total = total + in_ref[i].astype(f32)
-    rows = total.astype(bf16)
+    rows = jnp.concatenate(
+        [
+            total.astype(bf16),
+            jnp.zeros((place_ref.shape[0] - total.shape[0], columns), bf16),
+        ],
+        axis=0,
+    )
     picked = lax.dot_general(
         place_ref[...], rows, (((0,), (0,)), ((), ())), preferred_element_type=f32
     )
     weighted = (gate_ref[:, 0:1] * picked).astype(bf16)
-    row_score = jnp.sum(
-        weighted.astype(f32) * labels_ref[...].astype(f32), axis=1, keepdims=True
-    )
-    score_ref[...] = jnp.broadcast_to(row_score, (count, LANES))
+    for y in range(ny):
+        rows = slice(y * own_count, (y + 1) * own_count)
+        label = labels_ref[lax.rem(expert - y + ny, ny)].astype(f32)
+        row_score = jnp.sum(
+            weighted[rows].astype(f32) * label, axis=1, keepdims=True
+        )
+        score_ref[rows, :] = jnp.broadcast_to(row_score, (own_count, LANES))
     own = jnp.sum(
         res_ref[...].astype(f32) * own_ref[...].astype(f32), axis=1, keepdims=True
     )
@@ -266,22 +335,43 @@
         out_ref[y, :, columns:] = pads
 
 
-def out_kernel(in_ref, res_ref, out_ref, score_ref):
-    columns = out_ref.shape[1]
-    total = in_ref[0].astype(f32)
+def score_kernel(columns, in_ref, score_ref):
+    total = in_ref[0, :, columns:].astype(f32)
     for y in range(1, in_ref.shape[0]):
-        total = total + in_ref[y].astype(f32)
-    out_ref[...] = (res_ref[...].astype(f32) + total[:, :columns]).astype(bf16)
-    score = jnp.sum(total[:, columns:], axis=0, keepdims=True)
+        total = total + in_ref[y, :, columns:].astype(f32)
+    score = jnp.sum(total, axis=0, keepdims=True)
     for i in range(score_ref.shape[0]):
         score_ref[i] = score
 
 
+def out_kernel(in_ref, res_ref, out_ref):
+    columns = out_ref.shape[1]
+    total = in_ref[0, :, :columns].astype(f32)
+    for y in range(1, in_ref.shape[0]):
+        total = total + in_ref[y, :, :columns].astype(f32)
+    out_ref[...] = (res_ref[...].astype(f32) + total).astype(bf16)
+
+
+def margin_kernel(in_ref, slot_ref, ref_ref, out_ref):
+    total = in_ref[0]
+    for i in range(1, in_ref.shape[0]):
+        total = total + in_ref[i]
+    slots = slot_ref[...]
+    pair = lax.shift_right_logical(slots, 1)
+    polarity = (1 - 2 * (slots - 2 * pair)).astype(f32)
+    signed = polarity * (total[:, :SEQS] - ref_ref[...])
+    sums = [
+        jnp.sum(jnp.where(pair == p, signed, 0.0), axis=1, keepdims=True)
+        for p in range(PAIRS)
+    ]
+    out_ref[...] = dpo_beta * jnp.concatenate(sums, axis=1)
+
+
 def make_body(sizes):
     nx, nl, ny, nh, nc = sizes
 
-    def shifted(array, dz=0, dc=0):
-        return lax.ppermute(array, AXES, shift_pairs(sizes, dz, dc))
+    def shifted(array, **shift):
+        return lax.ppermute(array, AXES, shift_pairs(sizes, **shift))
 
     def body(
         tokens,
@@ -298,6 +388,7 @@
     ):
         count, width = tokens.shape
         half = width // nc
+        fold = half // 2
         columns = width // (nh * nc)
         own_count = count // ny
         units = w_gate.shape[2]
@@ -305,30 +396,40 @@
         own, own_far, place, gate, residual = call(
             functools.partial(front_kernel, own_count, columns),
             (
-                sds((nx, SLOTS, half), bf16),
-                sds((SLOTS, half), bf16),
-                sds((SLOTS, count), bf16),
+                sds((nx, 2 * SLOTS, fold), bf16),
+                sds((2 * SLOTS, fold), bf16),
+                sds((2 * SLOTS, count), bf16),
                 sds((count, LANES), f32),
                 sds((own_count, columns), bf16),
             ),
             (tokens, norm_gain[None, :], expert_ids.T, gate_weights.T),
+            in_specs=[HBM] * 4,
+            scratch=[
+                pltpu.VMEM((count, width), bf16),
+                pltpu.VMEM((1, width), f32),
+                pltpu.VMEM((2, count), jnp.int32),
+                pltpu.VMEM((2, count), f32),
+                pltpu.SemaphoreType.DMA((4,)),
+            ],
             spare=60,
         )
-        near = exchange(own, "x").reshape(nx * SLOTS, half)
+        near = exchange(own, "x")
         far = shifted(own_far, dz=2)
         w_send, w_mine = call(
             slice_kernel,
             (sds((2, half, units), bf16),) * 2,
             (w_gate, w_up),
-            in_specs=[ANY, ANY],
+            in_specs=[HBM, HBM],
             scratch=[pltpu.SemaphoreType.DMA((4,))],
             spare=60,
         )
         w_other = shifted(w_send, dc=1)
+        (near,) = call(pack_kernel, (sds((nx * SLOTS, half), bf16),), (near,))
         below = shifted(near, dz=1)
         above = shifted(near, dz=-1)
-        (far,) = call(far_kernel, (sds((nx, SLOTS, half), bf16),), (far,))
-        far = exchange(far, "x").reshape(nx * SLOTS, half)
+        (far,) = call(copies_kernel, (sds(own.shape, bf16),), (far,))
+        far = exchange(far, "x")
+        (far,) = call(pack_kernel, (sds((nx * SLOTS, half), bf16),), (far,))
         early_other = dots(near, far, w_other)
         early_mine = dots(near, far, w_mine)
         below, above, early_mine = lax.optimization_barrier((below, above, early_mine))
@@ -336,25 +437,30 @@
         theirs = shifted(other, dc=1)
         mine = dots(below, above, w_mine, early_mine)
         (hidden,) = call(
-            hidden_kernel, (sds((nx, nl, SLOTS, units), bf16),), (mine, theirs)
-        )
-        hidden = hidden.reshape(nx * nl * SLOTS, units)
-        labels = exchange(for_each(label_rows, ny), "y").reshape(count, columns)
-        before = shifted(hidden, dz=nl)
-        after = shifted(hidden, dz=-nl)
-        (mine,) = call(
-            stack_kernel, (sds((nh, *hidden.shape), bf16),), (hidden, after, before)
-        )
-        mine, labels = lax.optimization_barrier((mine, labels))
+            functools.partial(hidden_kernel, nx),
+            (sds((nh, nx * nl * SLOTS, units), bf16),),
+            (mine, theirs),
+        )
+        mine = exchange(hidden, "zh")
+        labels = label_rows[None]
+        while labels.shape[0] < ny:
+            size = labels.shape[0]
+            arrived = shifted(labels, dy=size)
+            (labels,) = call(
+                join_kernel,
+                (sds((2 * size, own_count, columns), bf16),),
+                (labels, arrived),
+            )
         others = shifted(mine, dc=1)
         (by_x,) = call(
-            functools.partial(down_kernel, nh),
+            down_kernel,
             (sds((nx, nl * SLOTS, columns), bf16),),
             (mine, others, w_down),
-            flops=2 * hidden.shape[0] * w_down.shape[1] * columns,
+            flops=2 * hidden.shape[1] * w_down.shape[1] * columns,
         )
         by_x = exchange(by_x, "x")
         (by_zl,) = call(sum_kernel, (sds((nl, SLOTS, columns), bf16),), (by_x,))
+        by_zl, labels = lax.optimization_barrier((by_zl, labels))
         by_zl = exchange(by_zl, "zl")
         (sent,) = call(
             mix_kernel,
@@ -363,23 +469,19 @@
             scratch=[pltpu.VMEM((count, LANES), f32)],
         )
         terms = exchange(sent, "y")
-        layer_out, partial_value = call(
-            out_kernel,
-            (sds((own_count, columns), bf16), sds((nh * nc, 1, LANES), f32)),
-            (terms, residual),
-        )
-        totals = exchange(partial_value, TENSOR)
-        totals = jnp.sum(totals, axis=(0, 1))[:SEQS]
-        slots_here = pair_slot[0]
-        polarity = (1 - 2 * (slots_here % 2)).astype(f32)
-        pair_member = (
-            (slots_here // 2)[:, None]
-            == jnp.arange(PAIRS, dtype=jnp.int32)[None, :]
-        ).astype(f32)
-        margins = dpo_beta * jnp.sum(
-            pair_member * (polarity * (totals - ref_scores[0]))[:, None], axis=0
-        )
-        return (layer_out, margins[None, :])
+        (score,) = call(
+            functools.partial(score_kernel, columns),
+            (sds((nh * nc, 1, LANES), f32),),
+            (terms,),
+        )
+        scores = exchange(score, TENSOR)
+        (layer_out,) = call(
+            out_kernel, (sds((own_count, columns), bf16),), (terms, residual)
+        )
+        (margins,) = call(
+            margin_kernel, (sds((1, PAIRS), f32),), (scores, pair_slot, ref_scores)
+        )
+        return (layer_out, margins)
 
     return body
 

time: 182 us -> 179 us (0.984)
  waiting for transfers between devices: 22.7 us -> 34.7 us
  starting transfers between devices: 67.6 us -> 58.9 us
  Pallas kernels: 22.7 us -> 19.2 us
  local copies, waits for them, and re-layouts: 2 us -> 0.05 us
    all_to_all x3, starting transfers between devices: 26.9 us -> 15.2 us  [exchange(): return lax.all_to_all(array, axis, 0, 0, tiled=True)]
    all_to_all x3, waiting for transfers between devices: 6.99 us -> 17.8 us  [exchange(): return lax.all_to_all(array, axis, 0, 0, tiled=True)]
    pallas_call x13 -> x19, Pallas kernels: 22.7 us -> 19.2 us  [call(): pl.pallas_call(kernel, out_shape=outs, in_specs=in_specs or [VMEM] * len(...]
    ppermute x8 -> x9, starting transfers between devices: 40.6 us -> 43.7 us  [shifted(): return lax.ppermute(array, AXES, shift_pairs(sizes, **shift))]
    ppermute x8 -> x9, waiting for transfers between devices: 15.7 us -> 16.9 us  [shifted(): return lax.ppermute(array, AXES, shift_pairs(sizes, **shift))]
  transfers between devices with their start and end apart: 11 -> 12, of which waited for: 5 -> 9; matrix products, arithmetic and copies ran while one was open for 0% -> 0% of each run, Pallas kernels for 7% -> 5%
where the time goes in v1:
time: 179 us; the launch traced here: 178 us
  blocking collectives  64 us (36%)
  starting transfers between devices  58.9 us (33%)
  waiting for transfers between devices  34.7 us (19%)
  Pallas kernels  19.2 us (11%)
    all_to_all x4, blocking collectives, exchange(): return lax.all_to_all(array, axis, 0, 0, tiled=True)  64 us
    ppermute x9, starting transfers between devices, shifted(): return lax.ppermute(array, AXES, shift_pairs(sizes, **shift))  43.7 us
    pallas_call x19, Pallas kernels, call(): pl.pallas_call(kernel, out_shape=outs, in_specs=in_specs or [VMEM] * len(...  19.2 us
    all_to_all x3, waiting for transfers between devices, exchange(): return lax.all_to_all(array, axis, 0, 0, tiled=True)  17.8 us
    ppermute x9, waiting for transfers between devices, shifted(): return lax.ppermute(array, AXES, shift_pairs(sizes, **shift))  16.9 us
    all_to_all x3, starting transfers between devices, exchange(): return lax.all_to_all(array, axis, 0, 0, tiled=True)  15.2 us
  transfers between devices with their start and end apart: 12, of which 9 were waited for; matrix products, arithmetic and copies ran while one was open for 0% of the time, Pallas kernels for 5%

profile of v1, /device:TPU:1, one launch (start us, length us, event | category | flops | bytes accessed | tf_op | source)
XLA Modules:
  0.0 177.8 jit_solution(11581142682569651776)
XLA Ops:
  0.6 3.5 %shard_map.126 = (bf16[2,3072,128]{2,1,0:T(8,128)(2,1)}, bf16[2,3072,128]{2,1,0:T(8,128)(2,1)}) custom-call(bf16[1,6144,128]{2,1,0:T(8,128)(2,1)} %gate_ref.1, bf16[1,6144,128]{2,1,0:T(8,128)(2,1)} %up_ref.1), custom_call_target="tpu_custom_call" | custom-call | flops 6291456 | bytes 6291456 | tf_op jit(solution)/shard_map/pallas_call | solution.py:55
  4.2 12.4 %collective-permute-start.3 = (bf16[2,3072,128]{2,1,0:T(8,128)(2,1)}, bf16[2,3072,128]{2,1,0:T(8,128)(2,1)S(1)}, u32[]{:S(2)}, u32[]{:S(2)}) collective-permute-start(bf16[2,3072,128]{2,1,0:T(8,128)(2,1)} %get-tuple-element.20), channel_id=1, source_target_pairs={{0,1},{1,0},{48,49},{49,48},{96,97},{97,96},{144,145},{145,144},{2... | collective-permute-start | bytes 4718600 | tf_op jit(solution)/shard_map/ppermute | solution.py:374
  16.5 3.1 %shard_map.122 = (bf16[4,72,1536]{2,1,0:T(8,128)(2,1)}, bf16[72,1536]{1,0:T(8,128)(2,1)}, bf16[72,128]{1,0:T(8,128)(2,1)}, f32[128,128]{1,0:T(8,128)}, bf16[16,1024]{1,0:T(8,128)(2,1)}) custom-call(bf16[128,6144]{1,0:T(8,128)(2,1)} %refs_0_.1, f32[1,6144]{1,0:T(1,128)} %bitcast.6, s32[2,128]{1,0:T(2,128)} %bitcast.7, f32[2,128]{1,0:T(2,128)} %bitcast.8), custom_call_target="tpu_custom_call" | custom-call | flops 2822144 | bytes 2822144 | tf_op jit(solution)/shard_map/pallas_call | solution.py:55
  19.7 3.6 %all-to-all-start = ((bf16[4,72,1536]{2,1,0:T(8,128)(2,1)}), bf16[4,72,1536]{2,1,0:T(8,128)(2,1)S(1)}, u32[]{:S(2)}, u32[]{:S(2)}) async-start(bf16[4,72,1536]{2,1,0:T(8,128)(2,1)} %get-tuple-element.14), calls=%async_computation | async-start | bytes 1769472 | tf_op jit(solution)/shard_map/all_to_all | solution.py:49
  23.3 1.9 %collective-permute-start.2 = (bf16[72,1536]{1,0:T(8,128)(2,1)S(1)}, bf16[72,1536]{1,0:T(8,128)(2,1)S(1)}, u32[]{:S(2)}, u32[]{:S(2)}) collective-permute-start(bf16[72,1536]{1,0:T(8,128)(2,1)S(1)} %copy-done.9), channel_id=1, source_target_pairs={{0,96},{1,97},{48,144},{49,145},{96,2},{97,3},{144,50},{145,51},{2... | collective-permute-start | bytes 663560 | tf_op jit(solution)/shard_map/ppermute | solution.py:374
  25.2 11.4 %all-to-all-done.in_ref = bf16[4,72,1536]{2,1,0:T(8,128)(2,1)S(1)} async-done(((bf16[4,72,1536]{2,1,0:T(8,128)(2,1)}), bf16[4,72,1536]{2,1,0:T(8,128)(2,1)S(1)}, u32[]{:S(2)}, u32[]{:S(2)}) %all-to-all-start) | async-done | bytes 884768 | tf_op jit(solution)/shard_map/all_to_all | solution.py:49
  37.3 1.9 %collective-permute-start = (bf16[144,3072]{1,0:T(8,128)(2,1)S(1)}, bf16[144,3072]{1,0:T(8,128)(2,1)S(1)}, u32[]{:S(2)}, u32[]{:S(2)}) collective-permute-start(bf16[144,3072]{1,0:T(8,128)(2,1)S(1)} %shard_map.123.a_ref), channel_id=1, source_target_pairs={{0,48},{1,49},{48,96},{49,97},{96,144},{97,145},{144,2},{145,3},{2... | collective-permute-start | bytes 2654216 | tf_op jit(solution)/shard_map/ppermute | solution.py:374
  39.3 5.6 %collective-permute-start.1 = (bf16[144,3072]{1,0:T(8,128)(2,1)S(1)}, bf16[144,3072]{1,0:T(8,128)(2,1)S(1)}, u32[]{:S(2)}, u32[]{:S(2)}) collective-permute-start(bf16[144,3072]{1,0:T(8,128)(2,1)S(1)} %shard_map.123.a_ref), channel_id=1, source_target_pairs={{0,148},{1,149},{48,0},{49,1},{96,48},{97,49},{144,96},{145,97},{2... | collective-permute-start | bytes 2654216 | tf_op jit(solution)/shard_map/ppermute | solution.py:374
  44.9 14.5 %all_to_all.35.in_ref = bf16[4,72,1536]{2,1,0:T(8,128)(2,1)S(1)} all-to-all(bf16[4,72,1536]{2,1,0:T(8,128)(2,1)S(1)} %shard_map.124), channel_id=1, replica_groups=mesh['x'=4,'zl'=4,'y'=8,'zh'=3,'c'=2] {'x'}, dimensions={0} | all-to-all | bytes 1769472 | tf_op jit(solution)/shard_map/all_to_all | solution.py:49
  59.4 0.6 shard_map.125.b_ref
  60.0 1.5 shard_map.127.refs_0_
  61.8 0.9 collective-permute-done.1.b_ref
  62.7 1.5 shard_map.129.refs_0_
  64.2 1.5 shard_map.130
  65.7 3.9 %collective-permute-start.4 = (f32[576,256]{1,0:T(8,128)S(1)}, f32[576,256]{1,0:T(8,128)S(1)}, u32[]{:S(2)}, u32[]{:S(2)}) collective-permute-start(f32[576,256]{1,0:T(8,128)S(1)} %shard_map.130), channel_id=1, source_target_pairs={{0,1},{1,0},{48,49},{49,48},{96,97},{97,96},{144,145},{145,144},{2... | collective-permute-start | bytes 1769480 | tf_op jit(solution)/shard_map/ppermute | solution.py:374
  69.6 1.5 shard_map.128.mine_ref
  71.7 19.3 %all_to_all.36.mine_ref = bf16[3,576,128]{2,1,0:T(8,128)(2,1)S(1)} all-to-all(bf16[3,576,128]{2,1,0:T(8,128)(2,1)S(1)} %shard_map.131), channel_id=1, replica_groups=mesh['x'=4,'zl'=4,'y'=8,'zh'=3,'c'=2] {'zh'}, dimensions={0} | all-to-all | bytes 884736 | tf_op jit(solution)/shard_map/all_to_all | solution.py:49
  91.0 5.3 %collective-permute-start.5 = (bf16[3,576,128]{2,1,0:T(8,128)(2,1)S(1)}, bf16[3,576,128]{2,1,0:T(8,128)(2,1)S(1)}, u32[]{:S(2)}, u32[]{:S(2)}) collective-permute-start(bf16[3,576,128]{2,1,0:T(8,128)(2,1)S(1)} %all_to_all.36.mine_ref), channel_id=1, source_target_pairs={{0,1},{1,0},{48,49},{49,48},{96,97},{97,96},{144,145},{145,144},{2... | collective-permute-start | bytes 1327112 | tf_op jit(solution)/shard_map/ppermute | solution.py:374
  96.3 1.4 collective-permute-done.5.other_ref
  97.7 2.1 %shard_map.132 = bf16[4,144,1024]{2,1,0:T(8,128)(2,1)} custom-call(bf16[3,576,128]{2,1,0:T(8,128)(2,1)S(1)} %all_to_all.36.mine_ref, bf16[3,576,128]{2,1,0:T(8,128)(2,1)S(1)} %collective-permute-done.5.other_ref, bf16[1,768,1024]{2,1,0:T(8,128)(2,1)S(1)} %copy-done.1), custom_call_target="tpu_custom_call" | custom-call | flops 905969664 | bytes 3637248 | tf_op jit(solution)/shard_map/pallas_call | solution.py:55
  99.8 3.7 %all-to-all-start.3 = ((bf16[4,144,1024]{2,1,0:T(8,128)(2,1)}), bf16[4,144,1024]{2,1,0:T(8,128)(2,1)S(1)}, u32[]{:S(2)}, u32[]{:S(2)}) async-start(bf16[4,144,1024]{2,1,0:T(8,128)(2,1)} %shard_map.132), calls=%async_computation.3 | async-start | bytes 2359296 | tf_op jit(solution)/shard_map/all_to_all | solution.py:49
  103.6 3.4 %collective-permute-start.6 = (bf16[1,16,1024]{2,1,0:T(8,128)(2,1)S(1)}, bf16[1,16,1024]{2,1,0:T(8,128)(2,1)S(1)}, u32[]{:S(2)}, u32[]{:S(2)}) collective-permute-start(bf16[1,16,1024]{2,1,0:T(8,128)(2,1)S(1)} %bitcast.4), channel_id=1, source_target_pairs={{0,6},{1,7},{48,54},{49,55},{96,102},{97,103},{144,150},{145,151},... | collective-permute-start | bytes 98312 | tf_op jit(solution)/shard_map/ppermute | solution.py:374
  107.0 3.5 %collective-permute-done.6.b_ref = bf16[1,16,1024]{2,1,0:T(8,128)(2,1)S(1)} collective-permute-done((bf16[1,16,1024]{2,1,0:T(8,128)(2,1)S(1)}, bf16[1,16,1024]{2,1,0:T(8,128)(2,1)S(1)}, u32[]{:S(2)}, u32[]{:S(2)}) %collective-permute-start.6) | collective-permute-done | bytes 32800 | tf_op jit(solution)/shard_map/ppermute | solution.py:374
  110.6 2.5 %collective-permute-start.7 = (bf16[2,16,1024]{2,1,0:T(8,128)(2,1)S(1)}, bf16[2,16,1024]{2,1,0:T(8,128)(2,1)S(1)}, u32[]{:S(2)}, u32[]{:S(2)}) collective-permute-start(bf16[2,16,1024]{2,1,0:T(8,128)(2,1)S(1)} %shard_map.134.a_ref), channel_id=1, source_target_pairs={{0,12},{1,13},{48,60},{49,61},{96,108},{97,109},{144,156},{145,157... | collective-permute-start | bytes 196616 | tf_op jit(solution)/shard_map/ppermute | solution.py:374
  113.0 5.6 %collective-permute-done.7.b_ref = bf16[2,16,1024]{2,1,0:T(8,128)(2,1)S(1)} collective-permute-done((bf16[2,16,1024]{2,1,0:T(8,128)(2,1)S(1)}, bf16[2,16,1024]{2,1,0:T(8,128)(2,1)S(1)}, u32[]{:S(2)}, u32[]{:S(2)}) %collective-permute-start.7) | collective-permute-done | bytes 65568 | tf_op jit(solution)/shard_map/ppermute | solution.py:374
  118.6 6.8 %collective-permute-start.8 = (bf16[4,16,1024]{2,1,0:T(8,128)(2,1)S(1)}, bf16[4,16,1024]{2,1,0:T(8,128)(2,1)S(1)}, u32[]{:S(2)}, u32[]{:S(2)}) collective-permute-start(bf16[4,16,1024]{2,1,0:T(8,128)(2,1)S(1)} %shard_map.135.a_ref), channel_id=1, source_target_pairs={{0,24},{1,25},{48,72},{49,73},{96,120},{97,121},{144,168},{145,169... | collective-permute-start | bytes 393224 | tf_op jit(solution)/shard_map/ppermute | solution.py:374
  125.4 5.1 %collective-permute-done.8.b_ref = bf16[4,16,1024]{2,1,0:T(8,128)(2,1)S(1)} collective-permute-done((bf16[4,16,1024]{2,1,0:T(8,128)(2,1)S(1)}, bf16[4,16,1024]{2,1,0:T(8,128)(2,1)S(1)}, u32[]{:S(2)}, u32[]{:S(2)}) %collective-permute-start.8) | collective-permute-done | bytes 131104 | tf_op jit(solution)/shard_map/ppermute | solution.py:374
  131.0 12.3 %all_to_all.37.in_ref = bf16[4,36,1024]{2,1,0:T(8,128)(2,1)S(1)} all-to-all(bf16[4,36,1024]{2,1,0:T(8,128)(2,1)S(1)} %shard_map.133), channel_id=1, replica_groups=mesh['x'=4,'zl'=4,'y'=8,'zh'=3,'c'=2] {'zl'}, dimensions={0} | all-to-all | bytes 589824 | tf_op jit(solution)/shard_map/all_to_all | solution.py:49
  143.7 18.0 %all_to_all.38.in_ref = bf16[8,16,1152]{2,1,0:T(8,128)(2,1)S(1)} all-to-all(bf16[8,16,1152]{2,1,0:T(8,128)(2,1)S(1)} %shard_map.137), channel_id=1, replica_groups=mesh['x'=4,'zl'=4,'y'=8,'zh'=3,'c'=2] {'y'}, dimensions={0} | all-to-all | bytes 589824 | tf_op jit(solution)/shard_map/all_to_all | solution.py:49
  162.3 7.9 %all-to-all-start.6 = ((f32[6,1,128]{2,1,0:T(1,128)}), f32[6,1,128]{2,1,0:T(1,128)S(1)}, u32[]{:S(2)}, u32[]{:S(2)}) async-start(f32[6,1,128]{2,1,0:T(1,128)} %shard_map.139), calls=%async_computation.6 | async-start | bytes 6144 | tf_op jit(solution)/shard_map/all_to_all | solution.py:49
  170.2 0.7 shard_map.138
  170.8 6.3 %all-to-all-done.6.in_ref = f32[6,1,128]{2,1,0:T(1,128)S(1)} async-done(((f32[6,1,128]{2,1,0:T(1,128)}), f32[6,1,128]{2,1,0:T(1,128)S(1)}, u32[]{:S(2)}, u32[]{:S(2)}) %all-to-all-start.6) | async-done | bytes 3104 | tf_op jit(solution)/shard_map/all_to_all | solution.py:49
  (35 shorter events, 3.7 us)
Async XLA Ops:
  4.2 58.5 %collective-permute-start.3 = (bf16[2,3072,128]{2,1,0:T(8,128)(2,1)}, bf16[2,3072,128]{2,1,0:T(8,128)(2,1)S(1)}, u32[]{:S(2)}, u32[]{:S(2)}) collective-permute-start(bf16[2,3072,128]{2,1,0:T(8,128)(2,1)} %get-tuple-element.20), channel_id=1, source_target_pairs={{0,1},{1,0},{48,49},{49,48},{96,97},{97,96},{144,145},{145,144},{2... | collective-permute-start | bytes 4718600 | tf_op jit(solution)/shard_map/ppermute | solution.py:374
  19.6 3.7 %copy-start.9 = (bf16[72,1536]{1,0:T(8,128)(2,1)S(1)}, bf16[72,1536]{1,0:T(8,128)(2,1)}, u32[]{:S(2)}) copy-start(bf16[72,1536]{1,0:T(8,128)(2,1)} %get-tuple-element.15) | copy-start | bytes 663556
  19.7 17.0 %all-to-all-start = ((bf16[4,72,1536]{2,1,0:T(8,128)(2,1)}), bf16[4,72,1536]{2,1,0:T(8,128)(2,1)S(1)}, u32[]{:S(2)}, u32[]{:S(2)}) async-start(bf16[4,72,1536]{2,1,0:T(8,128)(2,1)} %get-tuple-element.14), calls=%async_computation | async-start | bytes 1769472 | tf_op jit(solution)/shard_map/all_to_all | solution.py:49
  23.3 21.5 %collective-permute-start.2 = (bf16[72,1536]{1,0:T(8,128)(2,1)S(1)}, bf16[72,1536]{1,0:T(8,128)(2,1)S(1)}, u32[]{:S(2)}, u32[]{:S(2)}) collective-permute-start(bf16[72,1536]{1,0:T(8,128)(2,1)S(1)} %copy-done.9), channel_id=1, source_target_pairs={{0,96},{1,97},{48,144},{49,145},{96,2},{97,3},{144,50},{145,51},{2... | collective-permute-start | bytes 663560 | tf_op jit(solution)/shard_map/ppermute | solution.py:374
  37.3 24.5 %collective-permute-start = (bf16[144,3072]{1,0:T(8,128)(2,1)S(1)}, bf16[144,3072]{1,0:T(8,128)(2,1)S(1)}, u32[]{:S(2)}, u32[]{:S(2)}) collective-permute-start(bf16[144,3072]{1,0:T(8,128)(2,1)S(1)} %shard_map.123.a_ref), channel_id=1, source_target_pairs={{0,48},{1,49},{48,96},{49,97},{96,144},{97,145},{144,2},{145,3},{2... | collective-permute-start | bytes 2654216 | tf_op jit(solution)/shard_map/ppermute | solution.py:374
  39.3 23.4 %collective-permute-start.1 = (bf16[144,3072]{1,0:T(8,128)(2,1)S(1)}, bf16[144,3072]{1,0:T(8,128)(2,1)S(1)}, u32[]{:S(2)}, u32[]{:S(2)}) collective-permute-start(bf16[144,3072]{1,0:T(8,128)(2,1)S(1)} %shard_map.123.a_ref), channel_id=1, source_target_pairs={{0,148},{1,149},{48,0},{49,1},{96,48},{97,49},{144,96},{145,97},{2... | collective-permute-start | bytes 2654216 | tf_op jit(solution)/shard_map/ppermute | solution.py:374
  44.9 15.1 %copy-start = (bf16[2,3072,128]{2,1,0:T(8,128)(2,1)S(1)}, bf16[2,3072,128]{2,1,0:T(8,128)(2,1)}, u32[]{:S(2)}) copy-start(bf16[2,3072,128]{2,1,0:T(8,128)(2,1)} %get-tuple-element.16.w_ref) | copy-start | bytes 4718596
  65.7 5.5 %collective-permute-start.4 = (f32[576,256]{1,0:T(8,128)S(1)}, f32[576,256]{1,0:T(8,128)S(1)}, u32[]{:S(2)}, u32[]{:S(2)}) collective-permute-start(f32[576,256]{1,0:T(8,128)S(1)} %shard_map.130), channel_id=1, source_target_pairs={{0,1},{1,0},{48,49},{49,48},{96,97},{97,96},{144,145},{145,144},{2... | collective-permute-start | bytes 1769480 | tf_op jit(solution)/shard_map/ppermute | solution.py:374
  71.1 26.6 %copy-start.1 = (bf16[1,768,1024]{2,1,0:T(8,128)(2,1)S(1)}, bf16[1,768,1024]{2,1,0:T(8,128)(2,1)}, u32[]{:S(2)}) copy-start(bf16[1,768,1024]{2,1,0:T(8,128)(2,1)} %w_ref.1) | copy-start | bytes 4718596
  91.0 6.7 %collective-permute-start.5 = (bf16[3,576,128]{2,1,0:T(8,128)(2,1)S(1)}, bf16[3,576,128]{2,1,0:T(8,128)(2,1)S(1)}, u32[]{:S(2)}, u32[]{:S(2)}) collective-permute-start(bf16[3,576,128]{2,1,0:T(8,128)(2,1)S(1)} %all_to_all.36.mine_ref), channel_id=1, source_target_pairs={{0,1},{1,0},{48,49},{49,48},{96,97},{97,96},{144,145},{145,144},{2... | collective-permute-start | bytes 1327112 | tf_op jit(solution)/shard_map/ppermute | solution.py:374
  99.8 3.7 %copy-start.2 = (bf16[16,1024]{1,0:T(8,128)(2,1)S(1)}, bf16[16,1024]{1,0:T(8,128)(2,1)}, u32[]{:S(2)}) copy-start(bf16[16,1024]{1,0:T(8,128)(2,1)} %own_ref.1) | copy-start | bytes 98308
  99.8 30.7 %all-to-all-start.3 = ((bf16[4,144,1024]{2,1,0:T(8,128)(2,1)}), bf16[4,144,1024]{2,1,0:T(8,128)(2,1)S(1)}, u32[]{:S(2)}, u32[]{:S(2)}) async-start(bf16[4,144,1024]{2,1,0:T(8,128)(2,1)} %shard_map.132), calls=%async_computation.3 | async-start | bytes 2359296 | tf_op jit(solution)/shard_map/all_to_all | solution.py:49
  103.5 39.8 %copy-start.3 = (bf16[16,1024]{1,0:T(8,128)(2,1)S(1)}, bf16[16,1024]{1,0:T(8,128)(2,1)}, u32[]{:S(2)}) copy-start(bf16[16,1024]{1,0:T(8,128)(2,1)} %get-tuple-element.25.res_ref) | copy-start | bytes 98308
  103.5 39.7 %copy-start.4 = (f32[128,128]{1,0:T(8,128)S(1)}, f32[128,128]{1,0:T(8,128)}, u32[]{:S(2)}) copy-start(f32[128,128]{1,0:T(8,128)} %get-tuple-element.23.gate_ref) | copy-start | bytes 196612
  103.5 39.7 %copy-start.5 = (bf16[72,128]{1,0:T(8,128)(2,1)S(1)}, bf16[72,128]{1,0:T(8,128)(2,1)}, u32[]{:S(2)}) copy-start(bf16[72,128]{1,0:T(8,128)(2,1)} %get-tuple-element.22.place_ref) | copy-start | bytes 55300
  103.5 39.7 %copy-start.6 = (s32[1,128]{1,0:T(1,128)S(1)}, s32[1,128]{1,0:T(1,128)}, u32[]{:S(2)}) copy-start(s32[1,128]{1,0:T(1,128)} %seg_ref.1) | copy-start | bytes 1540
  103.6 7.0 %collective-permute-start.6 = (bf16[1,16,1024]{2,1,0:T(8,128)(2,1)S(1)}, bf16[1,16,1024]{2,1,0:T(8,128)(2,1)S(1)}, u32[]{:S(2)}, u32[]{:S(2)}) collective-permute-start(bf16[1,16,1024]{2,1,0:T(8,128)(2,1)S(1)} %bitcast.4), channel_id=1, source_target_pairs={{0,6},{1,7},{48,54},{49,55},{96,102},{97,103},{144,150},{145,151},... | collective-permute-start | bytes 98312 | tf_op jit(solution)/shard_map/ppermute | solution.py:374
  110.6 8.1 %collective-permute-start.7 = (bf16[2,16,1024]{2,1,0:T(8,128)(2,1)S(1)}, bf16[2,16,1024]{2,1,0:T(8,128)(2,1)S(1)}, u32[]{:S(2)}, u32[]{:S(2)}) collective-permute-start(bf16[2,16,1024]{2,1,0:T(8,128)(2,1)S(1)} %shard_map.134.a_ref), channel_id=1, source_target_pairs={{0,12},{1,13},{48,60},{49,61},{96,108},{97,109},{144,156},{145,157... | collective-permute-start | bytes 196616 | tf_op jit(solution)/shard_map/ppermute | solution.py:374
  118.6 11.9 %collective-permute-start.8 = (bf16[4,16,1024]{2,1,0:T(8,128)(2,1)S(1)}, bf16[4,16,1024]{2,1,0:T(8,128)(2,1)S(1)}, u32[]{:S(2)}, u32[]{:S(2)}) collective-permute-start(bf16[4,16,1024]{2,1,0:T(8,128)(2,1)S(1)} %shard_map.135.a_ref), channel_id=1, source_target_pairs={{0,24},{1,25},{48,72},{49,73},{96,120},{97,121},{144,168},{145,169... | collective-permute-start | bytes 393224 | tf_op jit(solution)/shard_map/ppermute | solution.py:374
  130.9 46.2 %copy-start.7 = (s32[1,4]{1,0:T(1,128)S(1)}, s32[1,4]{1,0:T(1,128)}, u32[]{:S(2)}) copy-start(s32[1,4]{1,0:T(1,128)} %slot_ref.1) | copy-start | bytes 52
  131.0 46.2 %copy-start.8 = (f32[1,4]{1,0:T(1,128)S(1)}, f32[1,4]{1,0:T(1,128)}, u32[]{:S(2)}) copy-start(f32[1,4]{1,0:T(1,128)} %ref_ref.1) | copy-start | bytes 52
  162.3 14.9 %all-to-all-start.6 = ((f32[6,1,128]{2,1,0:T(1,128)}), f32[6,1,128]{2,1,0:T(1,128)S(1)}, u32[]{:S(2)}, u32[]{:S(2)}) async-start(f32[6,1,128]{2,1,0:T(1,128)} %shard_map.139), calls=%async_computation.6 | async-start | bytes 6144 | tf_op jit(solution)/shard_map/all_to_all | solution.py:49

commit v2 on v1

--- a/solution.py
+++ b/solution.py
@@ -26,23 +26,27 @@
 HBM = pl.BlockSpec(memory_space=pltpu.HBM)
 
 
-def shift_pairs(sizes, dx=0, dy=0, dz=0, dc=0):
+def shift_pairs(sizes, dx=0, dy=0, dz=0, dc=0, cross=1):
     nx, nl, ny, nh, nc = sizes
     nz = nh * nl
 
     def flat(x, y, z, c):
         return (((x * nl + z % nl) * ny + y) * nh + z // nl) * nc + c
 
-    return [
-        (
-            flat(x, y, z, c),
-            flat((x + dx) % nx, (y + dy) % ny, (z + dz) % nz, (c + dc) % nc),
-        )
-        for x in range(nx)
-        for y in range(ny)
-        for z in range(nz)
-        for c in range(nc)
-    ]
+    pairs = []
+    for x in range(nx):
+        for y in range(ny):
+            for z in range(nz):
+                for c in range(nc):
+                    way = cross if c else 1
+                    target = flat(
+                        (x + way * dx) % nx,
+                        (y + dy) % ny,
+                        (z + way * dz) % nz,
+                        (c + dc) % nc,
+                    )
+                    pairs.append((flat(x, y, z, c), target))
+    return pairs
 
 
 def exchange(array, axis):
@@ -177,7 +181,7 @@
 
 def dots_kernel(a_ref, b_ref, w_ref, *refs):
     *first, out_ref, sum_ref = refs
-    _, half = a_ref.shape
+    rows, half = a_ref.shape
     step = 512
     sum_ref[...] = jnp.zeros_like(sum_ref)
 
@@ -197,7 +201,13 @@
     for ref in first:
         out_ref[at : at + ref.shape[0]] = ref[...]
         at += ref.shape[0]
-    out_ref[at:] = sum_ref[...]
+    if not first:
+        out_ref[...] = sum_ref[...]
+        return
+    core = lax.axis_index("c")
+    for i in range(2):
+        to = pl.multiple_of(at + lax.rem(core + i, 2) * rows, 16)
+        out_ref[pl.ds(to, rows), :] = sum_ref[i * rows : (i + 1) * rows]
 
 
 def dots(a, b, w, *first):
@@ -215,7 +225,7 @@
 
 
 def hidden_kernel(nx, mine_ref, theirs_ref, out_ref):
-    _, total, units = out_ref.shape
+    total, units = out_ref.shape
     block = total // nx
     parts = []
     for start in range(0, total, block):
@@ -233,18 +243,24 @@
             at = jnp.where(inside, source - base + r * SLOTS, at)
         chosen = jnp.where(at == slot, 1.0, 0.0).astype(bf16)
         moved = jnp.dot(chosen, hidden, preferred_element_type=f32)
-        moved = moved.astype(bf16)
-        for i in range(out_ref.shape[0]):
-            out_ref[i, x * block : (x + 1) * block] = moved
-
-
-def down_kernel(mine_ref, other_ref, w_ref, out_ref):
+        out_ref[x * block : (x + 1) * block] = moved.astype(bf16)
+
+
+def stack_kernel(own_ref, first_ref, second_ref, out_ref):
+    core = lax.axis_index("c")
+    out_ref[0] = own_ref[...]
+    out_ref[2 - core] = first_ref[...]
+    out_ref[1 + core] = second_ref[...]
+
+
+def down_kernel(nh, mine_ref, other_ref, w_ref, out_ref):
     nx, rows, _ = out_ref.shape
-    nh, _, units = mine_ref.shape
+    units = mine_ref.shape[2]
+    zh = lax.axis_index("zh")
     core = lax.axis_index("c")
     weights = []
     for step in range(nh):
-        base = step * 2
+        base = lax.rem(zh + step, nh) * 2
         weights.append(
             jnp.concatenate(
                 [
@@ -425,23 +441,29 @@
         )
         w_other = shifted(w_send, dc=1)
         (near,) = call(pack_kernel, (sds((nx * SLOTS, half), bf16),), (near,))
-        below = shifted(near, dz=1)
-        above = shifted(near, dz=-1)
+        first = shifted(near, dz=1, cross=-1)
+        second = shifted(near, dz=-1, cross=-1)
         (far,) = call(copies_kernel, (sds(own.shape, bf16),), (far,))
         far = exchange(far, "x")
         (far,) = call(pack_kernel, (sds((nx * SLOTS, half), bf16),), (far,))
         early_other = dots(near, far, w_other)
         early_mine = dots(near, far, w_mine)
-        below, above, early_mine = lax.optimization_barrier((below, above, early_mine))
-        other = dots(below, above, w_other, early_other)
+        first, second, early_mine = lax.optimization_barrier(
+            (first, second, early_mine)
+        )
+        other = dots(first, second, w_other, early_other)
         theirs = shifted(other, dc=1)
-        mine = dots(below, above, w_mine, early_mine)
+        mine = dots(first, second, w_mine, early_mine)
         (hidden,) = call(
             functools.partial(hidden_kernel, nx),
-            (sds((nh, nx * nl * SLOTS, units), bf16),),
+            (sds((nx * nl * SLOTS, units), bf16),),
             (mine, theirs),
         )
-        mine = exchange(hidden, "zh")
+        first = shifted(hidden, dz=nl, cross=-1)
+        second = shifted(hidden, dz=-nl, cross=-1)
+        (mine,) = call(
+            stack_kernel, (sds((nh, *hidden.shape), bf16),), (hidden, first, second)
+        )
         labels = label_rows[None]
         while labels.shape[0] < ny:
             size = labels.shape[0]
@@ -453,10 +475,10 @@
             )
         others = shifted(mine, dc=1)
         (by_x,) = call(
-            down_kernel,
+            functools.partial(down_kernel, nh),
             (sds((nx, nl * SLOTS, columns), bf16),),
             (mine, others, w_down),
-            flops=2 * hidden.shape[1] * w_down.shape[1] * columns,
+            flops=2 * hidden.shape[0] * w_down.shape[1] * columns,
         )
         by_x = exchange(by_x, "x")
         (by_zl,) = call(sum_kernel, (sds((nl, SLOTS, columns), bf16),), (by_x,))

time: 179 us -> 174 us (0.972)
  blocking collectives: 64 us -> 39.8 us
  waiting for transfers between devices: 34.7 us -> 52.2 us
  starting transfers between devices: 58.9 us -> 61.3 us
    all_to_all x4 -> x3, blocking collectives: 64 us -> 39.8 us  [exchange(): return lax.all_to_all(array, axis, 0, 0, tiled=True)]
    ppermute x9 -> x11, waiting for transfers between devices: 16.9 us -> 34.4 us  [shifted(): return lax.ppermute(array, AXES, shift_pairs(sizes, **shift))]
    ppermute x9 -> x11, starting transfers between devices: 43.7 us -> 47 us  [shifted(): return lax.ppermute(array, AXES, shift_pairs(sizes, **shift))]
    pallas_call x19 -> x20, Pallas kernels: 19.2 us -> 19.2 us  [call(): pl.pallas_call(kernel, out_shape=outs, in_specs=in_specs or [VMEM] * len(...]
  transfers between devices with their start and end apart: 12 -> 14, of which waited for: 9 -> 10; matrix products, arithmetic and copies ran while one was open for 0% -> 0% of each run, Pallas kernels for 5% -> 5%
where the time goes in v2:
time: 174 us
  starting transfers between devices  61.3 us (35%)
  waiting for transfers between devices  52.2 us (30%)
  blocking collectives  39.8 us (23%)
  Pallas kernels  19.2 us (11%)
    ppermute x11, starting transfers between devices, shifted(): return lax.ppermute(array, AXES, shift_pairs(sizes, **shift))  47 us
    all_to_all x3, blocking collectives, exchange(): return lax.all_to_all(array, axis, 0, 0, tiled=True)  39.8 us
    ppermute x11, waiting for transfers between devices, shifted(): return lax.ppermute(array, AXES, shift_pairs(sizes, **shift))  34.4 us
    pallas_call x20, Pallas kernels, call(): pl.pallas_call(kernel, out_shape=outs, in_specs=in_specs or [VMEM] * len(...  19.2 us
    all_to_all x3, waiting for transfers between devices, exchange(): return lax.all_to_all(array, axis, 0, 0, tiled=True)  17.8 us
    all_to_all x3, starting transfers between devices, exchange(): return lax.all_to_all(array, axis, 0, 0, tiled=True)  14.3 us
  transfers between devices with their start and end apart: 14, of which 10 were waited for; matrix products, arithmetic and copies ran while one was open for 0% of the time, Pallas kernels for 5%

profile of v2, /device:TPU:1, one launch (start us, length us, event | category | flops | bytes accessed | tf_op | source)
XLA Modules:
  0.0 173.6 jit_solution(8574498014745351229)
XLA Ops:
  0.6 3.5 %shard_map.126 = (bf16[2,3072,128]{2,1,0:T(8,128)(2,1)}, bf16[2,3072,128]{2,1,0:T(8,128)(2,1)}) custom-call(bf16[1,6144,128]{2,1,0:T(8,128)(2,1)} %gate_ref.1, bf16[1,6144,128]{2,1,0:T(8,128)(2,1)} %up_ref.1), custom_call_target="tpu_custom_call" | custom-call | flops 6291456 | bytes 6291456 | tf_op jit(solution)/shard_map/pallas_call | solution.py:59
  4.2 12.4 %collective-permute-start.3 = (bf16[2,3072,128]{2,1,0:T(8,128)(2,1)}, bf16[2,3072,128]{2,1,0:T(8,128)(2,1)S(1)}, u32[]{:S(2)}, u32[]{:S(2)}) collective-permute-start(bf16[2,3072,128]{2,1,0:T(8,128)(2,1)} %get-tuple-element.20), channel_id=1, source_target_pairs={{0,1},{1,0},{48,49},{49,48},{96,97},{97,96},{144,145},{145,144},{2... | collective-permute-start | bytes 4718600 | tf_op jit(solution)/shard_map/ppermute | solution.py:390
  16.6 3.1 %shard_map.122 = (bf16[4,72,1536]{2,1,0:T(8,128)(2,1)}, bf16[72,1536]{1,0:T(8,128)(2,1)}, bf16[72,128]{1,0:T(8,128)(2,1)}, f32[128,128]{1,0:T(8,128)}, bf16[16,1024]{1,0:T(8,128)(2,1)}) custom-call(bf16[128,6144]{1,0:T(8,128)(2,1)} %refs_0_.1, f32[1,6144]{1,0:T(1,128)} %bitcast.6, s32[2,128]{1,0:T(2,128)} %bitcast.7, f32[2,128]{1,0:T(2,128)} %bitcast.8), custom_call_target="tpu_custom_call" | custom-call | flops 2822144 | bytes 2822144 | tf_op jit(solution)/shard_map/pallas_call | solution.py:59
  19.7 3.6 %all-to-all-start = ((bf16[4,72,1536]{2,1,0:T(8,128)(2,1)}), bf16[4,72,1536]{2,1,0:T(8,128)(2,1)S(1)}, u32[]{:S(2)}, u32[]{:S(2)}) async-start(bf16[4,72,1536]{2,1,0:T(8,128)(2,1)} %get-tuple-element.14), calls=%async_computation | async-start | bytes 1769472 | tf_op jit(solution)/shard_map/all_to_all | solution.py:53
  23.3 1.9 %collective-permute-start.2 = (bf16[72,1536]{1,0:T(8,128)(2,1)S(1)}, bf16[72,1536]{1,0:T(8,128)(2,1)S(1)}, u32[]{:S(2)}, u32[]{:S(2)}) collective-permute-start(bf16[72,1536]{1,0:T(8,128)(2,1)S(1)} %copy-done.9), channel_id=1, source_target_pairs={{0,96},{1,97},{48,144},{49,145},{96,2},{97,3},{144,50},{145,51},{2... | collective-permute-start | bytes 663560 | tf_op jit(solution)/shard_map/ppermute | solution.py:390
  25.3 11.5 %all-to-all-done.in_ref = bf16[4,72,1536]{2,1,0:T(8,128)(2,1)S(1)} async-done(((bf16[4,72,1536]{2,1,0:T(8,128)(2,1)}), bf16[4,72,1536]{2,1,0:T(8,128)(2,1)S(1)}, u32[]{:S(2)}, u32[]{:S(2)}) %all-to-all-start) | async-done | bytes 884768 | tf_op jit(solution)/shard_map/all_to_all | solution.py:53
  37.4 5.6 %collective-permute-start = (bf16[144,3072]{1,0:T(8,128)(2,1)S(1)}, bf16[144,3072]{1,0:T(8,128)(2,1)S(1)}, u32[]{:S(2)}, u32[]{:S(2)}) collective-permute-start(bf16[144,3072]{1,0:T(8,128)(2,1)S(1)} %shard_map.123.a_ref), channel_id=1, source_target_pairs={{0,48},{1,149},{48,96},{49,1},{96,144},{97,49},{144,2},{145,97},{2... | collective-permute-start | bytes 2654216 | tf_op jit(solution)/shard_map/ppermute | solution.py:390
  42.9 1.9 %collective-permute-start.1 = (bf16[144,3072]{1,0:T(8,128)(2,1)S(1)}, bf16[144,3072]{1,0:T(8,128)(2,1)S(1)}, u32[]{:S(2)}, u32[]{:S(2)}) collective-permute-start(bf16[144,3072]{1,0:T(8,128)(2,1)S(1)} %shard_map.123.a_ref), channel_id=1, source_target_pairs={{0,148},{1,49},{48,0},{49,97},{96,48},{97,145},{144,96},{145,3},{2... | collective-permute-start | bytes 2654216 | tf_op jit(solution)/shard_map/ppermute | solution.py:390
  45.0 14.5 %all_to_all.30.in_ref = bf16[4,72,1536]{2,1,0:T(8,128)(2,1)S(1)} all-to-all(bf16[4,72,1536]{2,1,0:T(8,128)(2,1)S(1)} %shard_map.124), channel_id=1, replica_groups=mesh['x'=4,'zl'=4,'y'=8,'zh'=3,'c'=2] {'x'}, dimensions={0} | all-to-all | bytes 1769472 | tf_op jit(solution)/shard_map/all_to_all | solution.py:53
  61.5 2.6 %collective-permute-done.1.b_ref = bf16[144,3072]{1,0:T(8,128)(2,1)S(1)} collective-permute-done((bf16[144,3072]{1,0:T(8,128)(2,1)S(1)}, bf16[144,3072]{1,0:T(8,128)(2,1)S(1)}, u32[]{:S(2)}, u32[]{:S(2)}) %collective-permute-start.1) | collective-permute-done | bytes 884768 | tf_op jit(solution)/shard_map/ppermute | solution.py:390
  64.2 1.5 shard_map.129.refs_0_
  65.7 1.5 shard_map.130
  67.2 1.9 %collective-permute-start.4 = (f32[576,256]{1,0:T(8,128)S(1)}, f32[576,256]{1,0:T(8,128)S(1)}, u32[]{:S(2)}, u32[]{:S(2)}) collective-permute-start(f32[576,256]{1,0:T(8,128)S(1)} %shard_map.130), channel_id=1, source_target_pairs={{0,1},{1,0},{48,49},{49,48},{96,97},{97,96},{144,145},{145,144},{2... | collective-permute-start | bytes 1769480 | tf_op jit(solution)/shard_map/ppermute | solution.py:390
  69.1 1.5 shard_map.128.mine_ref
  71.5 4.8 %collective-permute-start.5 = (bf16[576,128]{1,0:T(8,128)(2,1)S(1)}, bf16[576,128]{1,0:T(8,128)(2,1)S(1)}, u32[]{:S(2)}, u32[]{:S(2)}) collective-permute-start(bf16[576,128]{1,0:T(8,128)(2,1)S(1)} %shard_map.131.own_ref), channel_id=1, source_target_pairs={{0,2},{1,5},{48,50},{49,53},{96,98},{97,101},{144,146},{145,149},{... | collective-permute-start | bytes 442376 | tf_op jit(solution)/shard_map/ppermute | solution.py:390
  76.3 4.4 %collective-permute-start.6 = (bf16[576,128]{1,0:T(8,128)(2,1)S(1)}, bf16[576,128]{1,0:T(8,128)(2,1)S(1)}, u32[]{:S(2)}, u32[]{:S(2)}) collective-permute-start(bf16[576,128]{1,0:T(8,128)(2,1)S(1)} %shard_map.131.own_ref), channel_id=1, source_target_pairs={{0,4},{1,3},{48,52},{49,51},{96,100},{97,99},{144,148},{145,147},{... | collective-permute-start | bytes 442376 | tf_op jit(solution)/shard_map/ppermute | solution.py:390
  80.7 2.0 %collective-permute-done.5.first_ref = bf16[576,128]{1,0:T(8,128)(2,1)S(1)} collective-permute-done((bf16[576,128]{1,0:T(8,128)(2,1)S(1)}, bf16[576,128]{1,0:T(8,128)(2,1)S(1)}, u32[]{:S(2)}, u32[]{:S(2)}) %collective-permute-start.5) | collective-permute-done | bytes 147488 | tf_op jit(solution)/shard_map/ppermute | solution.py:390
  82.7 11.0 %collective-permute-done.6.second_ref = bf16[576,128]{1,0:T(8,128)(2,1)S(1)} collective-permute-done((bf16[576,128]{1,0:T(8,128)(2,1)S(1)}, bf16[576,128]{1,0:T(8,128)(2,1)S(1)}, u32[]{:S(2)}, u32[]{:S(2)}) %collective-permute-start.6) | collective-permute-done | bytes 147488 | tf_op jit(solution)/shard_map/ppermute | solution.py:390
  93.8 1.9 %collective-permute-start.7 = (bf16[3,576,128]{2,1,0:T(8,128)(2,1)S(1)}, bf16[3,576,128]{2,1,0:T(8,128)(2,1)S(1)}, u32[]{:S(2)}, u32[]{:S(2)}) collective-permute-start(bf16[3,576,128]{2,1,0:T(8,128)(2,1)S(1)} %shard_map.132.mine_ref), channel_id=1, source_target_pairs={{0,1},{1,0},{48,49},{49,48},{96,97},{97,96},{144,145},{145,144},{2... | collective-permute-start | bytes 1327112 | tf_op jit(solution)/shard_map/ppermute | solution.py:390
  95.7 1.8 %collective-permute-done.7.other_ref = bf16[3,576,128]{2,1,0:T(8,128)(2,1)S(1)} collective-permute-done((bf16[3,576,128]{2,1,0:T(8,128)(2,1)S(1)}, bf16[3,576,128]{2,1,0:T(8,128)(2,1)S(1)}, u32[]{:S(2)}, u32[]{:S(2)}) %collective-permute-start.7) | collective-permute-done | bytes 442400 | tf_op jit(solution)/shard_map/ppermute | solution.py:390
  97.5 2.1 %shard_map.133 = bf16[4,144,1024]{2,1,0:T(8,128)(2,1)} custom-call(bf16[3,576,128]{2,1,0:T(8,128)(2,1)S(1)} %shard_map.132.mine_ref, bf16[3,576,128]{2,1,0:T(8,128)(2,1)S(1)} %collective-permute-done.7.other_ref, bf16[1,768,1024]{2,1,0:T(8,128)(2,1)S(1)} %copy-done.1), custom_call_target="tpu_custom_call" | custom-call | flops 905969664 | bytes 3637248 | tf_op jit(solution)/shard_map/pallas_call | solution.py:59
  99.6 3.7 %all-to-all-start.2 = ((bf16[4,144,1024]{2,1,0:T(8,128)(2,1)}), bf16[4,144,1024]{2,1,0:T(8,128)(2,1)S(1)}, u32[]{:S(2)}, u32[]{:S(2)}) async-start(bf16[4,144,1024]{2,1,0:T(8,128)(2,1)} %shard_map.133), calls=%async_computation.2 | async-start | bytes 2359296 | tf_op jit(solution)/shard_map/all_to_all | solution.py:53
  103.4 3.2 %collective-permute-start.8 = (bf16[1,16,1024]{2,1,0:T(8,128)(2,1)S(1)}, bf16[1,16,1024]{2,1,0:T(8,128)(2,1)S(1)}, u32[]{:S(2)}, u32[]{:S(2)}) collective-permute-start(bf16[1,16,1024]{2,1,0:T(8,128)(2,1)S(1)} %bitcast.4), channel_id=1, source_target_pairs={{0,6},{1,7},{48,54},{49,55},{96,102},{97,103},{144,150},{145,151},... | collective-permute-start | bytes 98312 | tf_op jit(solution)/shard_map/ppermute | solution.py:390
  106.6 3.6 %collective-permute-done.8.b_ref = bf16[1,16,1024]{2,1,0:T(8,128)(2,1)S(1)} collective-permute-done((bf16[1,16,1024]{2,1,0:T(8,128)(2,1)S(1)}, bf16[1,16,1024]{2,1,0:T(8,128)(2,1)S(1)}, u32[]{:S(2)}, u32[]{:S(2)}) %collective-permute-start.8) | collective-permute-done | bytes 32800 | tf_op jit(solution)/shard_map/ppermute | solution.py:390
  110.2 2.4 %collective-permute-start.9 = (bf16[2,16,1024]{2,1,0:T(8,128)(2,1)S(1)}, bf16[2,16,1024]{2,1,0:T(8,128)(2,1)S(1)}, u32[]{:S(2)}, u32[]{:S(2)}) collective-permute-start(bf16[2,16,1024]{2,1,0:T(8,128)(2,1)S(1)} %shard_map.135.a_ref), channel_id=1, source_target_pairs={{0,12},{1,13},{48,60},{49,61},{96,108},{97,109},{144,156},{145,157... | collective-permute-start | bytes 196616 | tf_op jit(solution)/shard_map/ppermute | solution.py:390
  112.6 5.9 %collective-permute-done.9.b_ref = bf16[2,16,1024]{2,1,0:T(8,128)(2,1)S(1)} collective-permute-done((bf16[2,16,1024]{2,1,0:T(8,128)(2,1)S(1)}, bf16[2,16,1024]{2,1,0:T(8,128)(2,1)S(1)}, u32[]{:S(2)}, u32[]{:S(2)}) %collective-permute-start.9) | collective-permute-done | bytes 65568 | tf_op jit(solution)/shard_map/ppermute | solution.py:390
  118.6 6.4 %collective-permute-start.10 = (bf16[4,16,1024]{2,1,0:T(8,128)(2,1)S(1)}, bf16[4,16,1024]{2,1,0:T(8,128)(2,1)S(1)}, u32[]{:S(2)}, u32[]{:S(2)}) collective-permute-start(bf16[4,16,1024]{2,1,0:T(8,128)(2,1)S(1)} %shard_map.136.a_ref), channel_id=1, source_target_pairs={{0,24},{1,25},{48,72},{49,73},{96,120},{97,121},{144,168},{145,169... | collective-permute-start | bytes 393224 | tf_op jit(solution)/shard_map/ppermute | solution.py:390
  125.0 7.1 %collective-permute-done.10.b_ref = bf16[4,16,1024]{2,1,0:T(8,128)(2,1)S(1)} collective-permute-done((bf16[4,16,1024]{2,1,0:T(8,128)(2,1)S(1)}, bf16[4,16,1024]{2,1,0:T(8,128)(2,1)S(1)}, u32[]{:S(2)}, u32[]{:S(2)}) %collective-permute-start.10) | collective-permute-done | bytes 131104 | tf_op jit(solution)/shard_map/ppermute | solution.py:390
  132.6 11.4 %all_to_all.31.in_ref = bf16[4,36,1024]{2,1,0:T(8,128)(2,1)S(1)} all-to-all(bf16[4,36,1024]{2,1,0:T(8,128)(2,1)S(1)} %shard_map.134), channel_id=1, replica_groups=mesh['x'=4,'zl'=4,'y'=8,'zh'=3,'c'=2] {'zl'}, dimensions={0} | all-to-all | bytes 589824 | tf_op jit(solution)/shard_map/all_to_all | solution.py:53
  144.4 13.9 %all_to_all.32.in_ref = bf16[8,16,1152]{2,1,0:T(8,128)(2,1)S(1)} all-to-all(bf16[8,16,1152]{2,1,0:T(8,128)(2,1)S(1)} %shard_map.138), channel_id=1, replica_groups=mesh['x'=4,'zl'=4,'y'=8,'zh'=3,'c'=2] {'y'}, dimensions={0} | all-to-all | bytes 589824 | tf_op jit(solution)/shard_map/all_to_all | solution.py:53
  159.0 7.0 %all-to-all-start.5 = ((f32[6,1,128]{2,1,0:T(1,128)}), f32[6,1,128]{2,1,0:T(1,128)S(1)}, u32[]{:S(2)}, u32[]{:S(2)}) async-start(f32[6,1,128]{2,1,0:T(1,128)} %shard_map.140), calls=%async_computation.5 | async-start | bytes 6144 | tf_op jit(solution)/shard_map/all_to_all | solution.py:53
  166.6 6.3 %all-to-all-done.5.in_ref = f32[6,1,128]{2,1,0:T(1,128)S(1)} async-done(((f32[6,1,128]{2,1,0:T(1,128)}), f32[6,1,128]{2,1,0:T(1,128)S(1)}, u32[]{:S(2)}, u32[]{:S(2)}) %all-to-all-start.5) | async-done | bytes 3104 | tf_op jit(solution)/shard_map/all_to_all | solution.py:53
  (39 shorter events, 6.5 us)
Async XLA Ops:
  4.2 60.0 %collective-permute-start.3 = (bf16[2,3072,128]{2,1,0:T(8,128)(2,1)}, bf16[2,3072,128]{2,1,0:T(8,128)(2,1)S(1)}, u32[]{:S(2)}, u32[]{:S(2)}) collective-permute-start(bf16[2,3072,128]{2,1,0:T(8,128)(2,1)} %get-tuple-element.20), channel_id=1, source_target_pairs={{0,1},{1,0},{48,49},{49,48},{96,97},{97,96},{144,145},{145,144},{2... | collective-permute-start | bytes 4718600 | tf_op jit(solution)/shard_map/ppermute | solution.py:390
  19.7 3.7 %copy-start.9 = (bf16[72,1536]{1,0:T(8,128)(2,1)S(1)}, bf16[72,1536]{1,0:T(8,128)(2,1)}, u32[]{:S(2)}) copy-start(bf16[72,1536]{1,0:T(8,128)(2,1)} %get-tuple-element.15) | copy-start | bytes 663556
  19.7 17.0 %all-to-all-start = ((bf16[4,72,1536]{2,1,0:T(8,128)(2,1)}), bf16[4,72,1536]{2,1,0:T(8,128)(2,1)S(1)}, u32[]{:S(2)}, u32[]{:S(2)}) async-start(bf16[4,72,1536]{2,1,0:T(8,128)(2,1)} %get-tuple-element.14), calls=%async_computation | async-start | bytes 1769472 | tf_op jit(solution)/shard_map/all_to_all | solution.py:53
  23.3 21.5 %collective-permute-start.2 = (bf16[72,1536]{1,0:T(8,128)(2,1)S(1)}, bf16[72,1536]{1,0:T(8,128)(2,1)S(1)}, u32[]{:S(2)}, u32[]{:S(2)}) collective-permute-start(bf16[72,1536]{1,0:T(8,128)(2,1)S(1)} %copy-done.9), channel_id=1, source_target_pairs={{0,96},{1,97},{48,144},{49,145},{96,2},{97,3},{144,50},{145,51},{2... | collective-permute-start | bytes 663560 | tf_op jit(solution)/shard_map/ppermute | solution.py:390
  37.4 24.2 %collective-permute-start = (bf16[144,3072]{1,0:T(8,128)(2,1)S(1)}, bf16[144,3072]{1,0:T(8,128)(2,1)S(1)}, u32[]{:S(2)}, u32[]{:S(2)}) collective-permute-start(bf16[144,3072]{1,0:T(8,128)(2,1)S(1)} %shard_map.123.a_ref), channel_id=1, source_target_pairs={{0,48},{1,149},{48,96},{49,1},{96,144},{97,49},{144,2},{145,97},{2... | collective-permute-start | bytes 2654216 | tf_op jit(solution)/shard_map/ppermute | solution.py:390
  42.9 21.2 %collective-permute-start.1 = (bf16[144,3072]{1,0:T(8,128)(2,1)S(1)}, bf16[144,3072]{1,0:T(8,128)(2,1)S(1)}, u32[]{:S(2)}, u32[]{:S(2)}) collective-permute-start(bf16[144,3072]{1,0:T(8,128)(2,1)S(1)} %shard_map.123.a_ref), channel_id=1, source_target_pairs={{0,148},{1,49},{48,0},{49,97},{96,48},{97,145},{144,96},{145,3},{2... | collective-permute-start | bytes 2654216 | tf_op jit(solution)/shard_map/ppermute | solution.py:390
  44.9 15.1 %copy-start = (bf16[2,3072,128]{2,1,0:T(8,128)(2,1)S(1)}, bf16[2,3072,128]{2,1,0:T(8,128)(2,1)}, u32[]{:S(2)}) copy-start(bf16[2,3072,128]{2,1,0:T(8,128)(2,1)} %get-tuple-element.16.w_ref) | copy-start | bytes 4718596
  67.2 3.9 %collective-permute-start.4 = (f32[576,256]{1,0:T(8,128)S(1)}, f32[576,256]{1,0:T(8,128)S(1)}, u32[]{:S(2)}, u32[]{:S(2)}) collective-permute-start(f32[576,256]{1,0:T(8,128)S(1)} %shard_map.130), channel_id=1, source_target_pairs={{0,1},{1,0},{48,49},{49,48},{96,97},{97,96},{144,145},{145,144},{2... | collective-permute-start | bytes 1769480 | tf_op jit(solution)/shard_map/ppermute | solution.py:390
  70.6 26.9 %copy-start.1 = (bf16[1,768,1024]{2,1,0:T(8,128)(2,1)S(1)}, bf16[1,768,1024]{2,1,0:T(8,128)(2,1)}, u32[]{:S(2)}) copy-start(bf16[1,768,1024]{2,1,0:T(8,128)(2,1)} %w_ref.1) | copy-start | bytes 4718596
  71.5 11.2 %collective-permute-start.5 = (bf16[576,128]{1,0:T(8,128)(2,1)S(1)}, bf16[576,128]{1,0:T(8,128)(2,1)S(1)}, u32[]{:S(2)}, u32[]{:S(2)}) collective-permute-start(bf16[576,128]{1,0:T(8,128)(2,1)S(1)} %shard_map.131.own_ref), channel_id=1, source_target_pairs={{0,2},{1,5},{48,50},{49,53},{96,98},{97,101},{144,146},{145,149},{... | collective-permute-start | bytes 442376 | tf_op jit(solution)/shard_map/ppermute | solution.py:390
  76.3 17.4 %collective-permute-start.6 = (bf16[576,128]{1,0:T(8,128)(2,1)S(1)}, bf16[576,128]{1,0:T(8,128)(2,1)S(1)}, u32[]{:S(2)}, u32[]{:S(2)}) collective-permute-start(bf16[576,128]{1,0:T(8,128)(2,1)S(1)} %shard_map.131.own_ref), channel_id=1, source_target_pairs={{0,4},{1,3},{48,52},{49,51},{96,100},{97,99},{144,148},{145,147},{... | collective-permute-start | bytes 442376 | tf_op jit(solution)/shard_map/ppermute | solution.py:390
  93.8 3.7 %collective-permute-start.7 = (bf16[3,576,128]{2,1,0:T(8,128)(2,1)S(1)}, bf16[3,576,128]{2,1,0:T(8,128)(2,1)S(1)}, u32[]{:S(2)}, u32[]{:S(2)}) collective-permute-start(bf16[3,576,128]{2,1,0:T(8,128)(2,1)S(1)} %shard_map.132.mine_ref), channel_id=1, source_target_pairs={{0,1},{1,0},{48,49},{49,48},{96,97},{97,96},{144,145},{145,144},{2... | collective-permute-start | bytes 1327112 | tf_op jit(solution)/shard_map/ppermute | solution.py:390
  99.6 3.7 %copy-start.2 = (bf16[16,1024]{1,0:T(8,128)(2,1)S(1)}, bf16[16,1024]{1,0:T(8,128)(2,1)}, u32[]{:S(2)}) copy-start(bf16[16,1024]{1,0:T(8,128)(2,1)} %own_ref.1) | copy-start | bytes 98308
  99.6 32.5 %all-to-all-start.2 = ((bf16[4,144,1024]{2,1,0:T(8,128)(2,1)}), bf16[4,144,1024]{2,1,0:T(8,128)(2,1)S(1)}, u32[]{:S(2)}, u32[]{:S(2)}) async-start(bf16[4,144,1024]{2,1,0:T(8,128)(2,1)} %shard_map.133), calls=%async_computation.2 | async-start | bytes 2359296 | tf_op jit(solution)/shard_map/all_to_all | solution.py:53
  103.3 40.7 %copy-start.3 = (bf16[16,1024]{1,0:T(8,128)(2,1)S(1)}, bf16[16,1024]{1,0:T(8,128)(2,1)}, u32[]{:S(2)}) copy-start(bf16[16,1024]{1,0:T(8,128)(2,1)} %get-tuple-element.25.res_ref) | copy-start | bytes 98308
  103.3 40.7 %copy-start.4 = (f32[128,128]{1,0:T(8,128)S(1)}, f32[128,128]{1,0:T(8,128)}, u32[]{:S(2)}) copy-start(f32[128,128]{1,0:T(8,128)} %get-tuple-element.23.gate_ref) | copy-start | bytes 196612
  103.3 40.6 %copy-start.5 = (bf16[72,128]{1,0:T(8,128)(2,1)S(1)}, bf16[72,128]{1,0:T(8,128)(2,1)}, u32[]{:S(2)}) copy-start(bf16[72,128]{1,0:T(8,128)(2,1)} %get-tuple-element.22.place_ref) | copy-start | bytes 55300
  103.3 40.6 %copy-start.6 = (s32[1,128]{1,0:T(1,128)S(1)}, s32[1,128]{1,0:T(1,128)}, u32[]{:S(2)}) copy-start(s32[1,128]{1,0:T(1,128)} %seg_ref.1) | copy-start | bytes 1540
  103.4 6.8 %collective-permute-start.8 = (bf16[1,16,1024]{2,1,0:T(8,128)(2,1)S(1)}, bf16[1,16,1024]{2,1,0:T(8,128)(2,1)S(1)}, u32[]{:S(2)}, u32[]{:S(2)}) collective-permute-start(bf16[1,16,1024]{2,1,0:T(8,128)(2,1)S(1)} %bitcast.4), channel_id=1, source_target_pairs={{0,6},{1,7},{48,54},{49,55},{96,102},{97,103},{144,150},{145,151},... | collective-permute-start | bytes 98312 | tf_op jit(solution)/shard_map/ppermute | solution.py:390
  110.2 8.4 %collective-permute-start.9 = (bf16[2,16,1024]{2,1,0:T(8,128)(2,1)S(1)}, bf16[2,16,1024]{2,1,0:T(8,128)(2,1)S(1)}, u32[]{:S(2)}, u32[]{:S(2)}) collective-permute-start(bf16[2,16,1024]{2,1,0:T(8,128)(2,1)S(1)} %shard_map.135.a_ref), channel_id=1, source_target_pairs={{0,12},{1,13},{48,60},{49,61},{96,108},{97,109},{144,156},{145,157... | collective-permute-start | bytes 196616 | tf_op jit(solution)/shard_map/ppermute | solution.py:390
  118.6 13.5 %collective-permute-start.10 = (bf16[4,16,1024]{2,1,0:T(8,128)(2,1)S(1)}, bf16[4,16,1024]{2,1,0:T(8,128)(2,1)S(1)}, u32[]{:S(2)}, u32[]{:S(2)}) collective-permute-start(bf16[4,16,1024]{2,1,0:T(8,128)(2,1)S(1)} %shard_map.136.a_ref), channel_id=1, source_target_pairs={{0,24},{1,25},{48,72},{49,73},{96,120},{97,121},{144,168},{145,169... | collective-permute-start | bytes 393224 | tf_op jit(solution)/shard_map/ppermute | solution.py:390
  132.5 40.4 %copy-start.7 = (s32[1,4]{1,0:T(1,128)S(1)}, s32[1,4]{1,0:T(1,128)}, u32[]{:S(2)}) copy-start(s32[1,4]{1,0:T(1,128)} %slot_ref.1) | copy-start | bytes 52
  132.5 40.4 %copy-start.8 = (f32[1,4]{1,0:T(1,128)S(1)}, f32[1,4]{1,0:T(1,128)}, u32[]{:S(2)}) copy-start(f32[1,4]{1,0:T(1,128)} %ref_ref.1) | copy-start | bytes 52
  159.0 14.0 %all-to-all-start.5 = ((f32[6,1,128]{2,1,0:T(1,128)}), f32[6,1,128]{2,1,0:T(1,128)S(1)}, u32[]{:S(2)}, u32[]{:S(2)}) async-start(f32[6,1,128]{2,1,0:T(1,128)} %shard_map.140), calls=%async_computation.5 | async-start | bytes 6144 | tf_op jit(solution)/shard_map/all_to_all | solution.py:53

commit v3 on v2

--- a/solution.py
+++ b/solution.py
@@ -75,26 +75,29 @@
 
 def front_kernel(own_count, columns, *refs):
     *ins, own_ref, far_ref, place_ref, gate_ref, res_ref, tok_ref, gain_ref, ids_ref, gw_ref, sems = refs
-    copies = [
+    count, width = tok_ref.shape
+    quarter = width // 4
+    small = [
         pltpu.make_async_copy(ref, held, sems.at[i])
         for i, (ref, held) in enumerate(
-            zip(ins, (tok_ref, gain_ref, ids_ref, gw_ref), strict=True)
+            zip(ins[1:], (gain_ref, ids_ref, gw_ref), strict=True)
         )
     ]
-    for copy in copies:
+    large = [
+        pltpu.make_async_copy(
+            ins[0].at[:, pl.ds(i * quarter, quarter)],
+            tok_ref.at[:, pl.ds(i * quarter, quarter)],
+            sems.at[3 + i],
+        )
+        for i in range(4)
+    ]
+    for copy in small[1:] + large + small[:1]:
         copy.start()
-    for copy in copies:
+    for copy in small[1:]:
         copy.wait()
-    count, width = tok_ref.shape
     expert = lax.axis_index("y")
     core = lax.axis_index("c")
     step = 512
-    squares = jnp.zeros((count, step), f32)
-    for start in range(0, width, step):
-        v = tok_ref[:, start : start + step].astype(f32)
-        squares = squares + v * v
-    total = jnp.sum(squares, axis=1, keepdims=True)
-    inverse_rms = lax.rsqrt(total * (1.0 / width) + epsilon)
     match = ids_ref[...] == expert
     hit = match.astype(f32)
     named = hit[0:1] + hit[1:2]
@@ -112,6 +115,15 @@
     upper = jnp.where((slot == position) & here, 1.0, 0.0).astype(bf16)
     lower = jnp.where((slot - SLOTS == position) & here, 1.0, 0.0).astype(bf16)
     place_ref[...] = upper
+    squares = jnp.zeros((count, step), f32)
+    for start in range(0, width, step):
+        if start % quarter == 0:
+            large[start // quarter].wait()
+        v = tok_ref[:, start : start + step].astype(f32)
+        squares = squares + v * v
+    total = jnp.sum(squares, axis=1, keepdims=True)
+    inverse_rms = lax.rsqrt(total * (1.0 / width) + epsilon)
+    small[0].wait()
     fold = own_ref.shape[2]
     half = 2 * fold
     nc = width // half
@@ -425,7 +437,7 @@
                 pltpu.VMEM((1, width), f32),
                 pltpu.VMEM((2, count), jnp.int32),
                 pltpu.VMEM((2, count), f32),
-                pltpu.SemaphoreType.DMA((4,)),
+                pltpu.SemaphoreType.DMA((7,)),
             ],
             spare=60,
         )

time: 174 us -> 175 us (level)
  no operation moved by 1% of the time
where the time goes in v3:
time: 175 us; the launch traced here: 174 us
  starting transfers between devices  61.6 us (35%)
  waiting for transfers between devices  51.8 us (30%)
  blocking collectives  40.4 us (23%)
  Pallas kernels  19.1 us (11%)
    ppermute x11, starting transfers between devices, shifted(): return lax.ppermute(array, AXES, shift_pairs(sizes, **shift))  47.2 us
    all_to_all x3, blocking collectives, exchange(): return lax.all_to_all(array, axis, 0, 0, tiled=True)  40.4 us
    ppermute x11, waiting for transfers between devices, shifted(): return lax.ppermute(array, AXES, shift_pairs(sizes, **shift))  34 us
    pallas_call x20, Pallas kernels, call(): pl.pallas_call(kernel, out_shape=outs, in_specs=in_specs or [VMEM] * len(...  19.1 us
    all_to_all x3, waiting for transfers between devices, exchange(): return lax.all_to_all(array, axis, 0, 0, tiled=True)  17.8 us
    all_to_all x3, starting transfers between devices, exchange(): return lax.all_to_all(array, axis, 0, 0, tiled=True)  14.3 us
  transfers between devices with their start and end apart: 14, of which 10 were waited for; matrix products, arithmetic and copies ran while one was open for 0% of the time, Pallas kernels for 5%

profile of v3, /device:TPU:1, one launch (start us, length us, event | category | flops | bytes accessed | tf_op | source)
XLA Modules:
  0.0 173.8 jit_solution(11038356434472526126)
XLA Ops:
  0.6 3.5 %shard_map.126 = (bf16[2,3072,128]{2,1,0:T(8,128)(2,1)}, bf16[2,3072,128]{2,1,0:T(8,128)(2,1)}) custom-call(bf16[1,6144,128]{2,1,0:T(8,128)(2,1)} %gate_ref.1, bf16[1,6144,128]{2,1,0:T(8,128)(2,1)} %up_ref.1), custom_call_target="tpu_custom_call" | custom-call | flops 6291456 | bytes 6291456 | tf_op jit(solution)/shard_map/pallas_call | solution.py:59
  4.2 12.4 %collective-permute-start.3 = (bf16[2,3072,128]{2,1,0:T(8,128)(2,1)}, bf16[2,3072,128]{2,1,0:T(8,128)(2,1)S(1)}, u32[]{:S(2)}, u32[]{:S(2)}) collective-permute-start(bf16[2,3072,128]{2,1,0:T(8,128)(2,1)} %get-tuple-element.20), channel_id=1, source_target_pairs={{0,1},{1,0},{48,49},{49,48},{96,97},{97,96},{144,145},{145,144},{2... | collective-permute-start | bytes 4718600 | tf_op jit(solution)/shard_map/ppermute | solution.py:402
  16.6 3.0 %shard_map.122 = (bf16[4,72,1536]{2,1,0:T(8,128)(2,1)}, bf16[72,1536]{1,0:T(8,128)(2,1)}, bf16[72,128]{1,0:T(8,128)(2,1)}, f32[128,128]{1,0:T(8,128)}, bf16[16,1024]{1,0:T(8,128)(2,1)}) custom-call(bf16[128,6144]{1,0:T(8,128)(2,1)} %refs_0_.1, f32[1,6144]{1,0:T(1,128)} %bitcast.6, s32[2,128]{1,0:T(2,128)} %bitcast.7, f32[2,128]{1,0:T(2,128)} %bitcast.8), custom_call_target="tpu_custom_call" | custom-call | flops 2822144 | bytes 2822144 | tf_op jit(solution)/shard_map/pallas_call | solution.py:59
  19.6 3.6 %all-to-all-start = ((bf16[4,72,1536]{2,1,0:T(8,128)(2,1)}), bf16[4,72,1536]{2,1,0:T(8,128)(2,1)S(1)}, u32[]{:S(2)}, u32[]{:S(2)}) async-start(bf16[4,72,1536]{2,1,0:T(8,128)(2,1)} %get-tuple-element.14), calls=%async_computation | async-start | bytes 1769472 | tf_op jit(solution)/shard_map/all_to_all | solution.py:53
  23.2 1.9 %collective-permute-start.2 = (bf16[72,1536]{1,0:T(8,128)(2,1)S(1)}, bf16[72,1536]{1,0:T(8,128)(2,1)S(1)}, u32[]{:S(2)}, u32[]{:S(2)}) collective-permute-start(bf16[72,1536]{1,0:T(8,128)(2,1)S(1)} %copy-done.9), channel_id=1, source_target_pairs={{0,96},{1,97},{48,144},{49,145},{96,2},{97,3},{144,50},{145,51},{2... | collective-permute-start | bytes 663560 | tf_op jit(solution)/shard_map/ppermute | solution.py:402
  25.1 11.4 %all-to-all-done.in_ref = bf16[4,72,1536]{2,1,0:T(8,128)(2,1)S(1)} async-done(((bf16[4,72,1536]{2,1,0:T(8,128)(2,1)}), bf16[4,72,1536]{2,1,0:T(8,128)(2,1)S(1)}, u32[]{:S(2)}, u32[]{:S(2)}) %all-to-all-start) | async-done | bytes 884768 | tf_op jit(solution)/shard_map/all_to_all | solution.py:53
  37.2 5.6 %collective-permute-start = (bf16[144,3072]{1,0:T(8,128)(2,1)S(1)}, bf16[144,3072]{1,0:T(8,128)(2,1)S(1)}, u32[]{:S(2)}, u32[]{:S(2)}) collective-permute-start(bf16[144,3072]{1,0:T(8,128)(2,1)S(1)} %shard_map.123.a_ref), channel_id=1, source_target_pairs={{0,48},{1,149},{48,96},{49,1},{96,144},{97,49},{144,2},{145,97},{2... | collective-permute-start | bytes 2654216 | tf_op jit(solution)/shard_map/ppermute | solution.py:402
  42.8 1.9 %collective-permute-start.1 = (bf16[144,3072]{1,0:T(8,128)(2,1)S(1)}, bf16[144,3072]{1,0:T(8,128)(2,1)S(1)}, u32[]{:S(2)}, u32[]{:S(2)}) collective-permute-start(bf16[144,3072]{1,0:T(8,128)(2,1)S(1)} %shard_map.123.a_ref), channel_id=1, source_target_pairs={{0,148},{1,49},{48,0},{49,97},{96,48},{97,145},{144,96},{145,3},{2... | collective-permute-start | bytes 2654216 | tf_op jit(solution)/shard_map/ppermute | solution.py:402
  44.8 14.5 %all_to_all.30.in_ref = bf16[4,72,1536]{2,1,0:T(8,128)(2,1)S(1)} all-to-all(bf16[4,72,1536]{2,1,0:T(8,128)(2,1)S(1)} %shard_map.124), channel_id=1, replica_groups=mesh['x'=4,'zl'=4,'y'=8,'zh'=3,'c'=2] {'x'}, dimensions={0} | all-to-all | bytes 1769472 | tf_op jit(solution)/shard_map/all_to_all | solution.py:53
  59.9 1.5 shard_map.127.refs_0_
  61.4 2.6 %collective-permute-done.1.b_ref = bf16[144,3072]{1,0:T(8,128)(2,1)S(1)} collective-permute-done((bf16[144,3072]{1,0:T(8,128)(2,1)S(1)}, bf16[144,3072]{1,0:T(8,128)(2,1)S(1)}, u32[]{:S(2)}, u32[]{:S(2)}) %collective-permute-start.1) | collective-permute-done | bytes 884768 | tf_op jit(solution)/shard_map/ppermute | solution.py:402
  65.5 1.5 shard_map.130
  67.0 1.9 %collective-permute-start.4 = (f32[576,256]{1,0:T(8,128)S(1)}, f32[576,256]{1,0:T(8,128)S(1)}, u32[]{:S(2)}, u32[]{:S(2)}) collective-permute-start(f32[576,256]{1,0:T(8,128)S(1)} %shard_map.130), channel_id=1, source_target_pairs={{0,1},{1,0},{48,49},{49,48},{96,97},{97,96},{144,145},{145,144},{2... | collective-permute-start | bytes 1769480 | tf_op jit(solution)/shard_map/ppermute | solution.py:402
  69.0 1.5 shard_map.128.mine_ref
  71.4 4.8 %collective-permute-start.5 = (bf16[576,128]{1,0:T(8,128)(2,1)S(1)}, bf16[576,128]{1,0:T(8,128)(2,1)S(1)}, u32[]{:S(2)}, u32[]{:S(2)}) collective-permute-start(bf16[576,128]{1,0:T(8,128)(2,1)S(1)} %shard_map.131.own_ref), channel_id=1, source_target_pairs={{0,2},{1,5},{48,50},{49,53},{96,98},{97,101},{144,146},{145,149},{... | collective-permute-start | bytes 442376 | tf_op jit(solution)/shard_map/ppermute | solution.py:402
  76.2 4.4 %collective-permute-start.6 = (bf16[576,128]{1,0:T(8,128)(2,1)S(1)}, bf16[576,128]{1,0:T(8,128)(2,1)S(1)}, u32[]{:S(2)}, u32[]{:S(2)}) collective-permute-start(bf16[576,128]{1,0:T(8,128)(2,1)S(1)} %shard_map.131.own_ref), channel_id=1, source_target_pairs={{0,4},{1,3},{48,52},{49,51},{96,100},{97,99},{144,148},{145,147},{... | collective-permute-start | bytes 442376 | tf_op jit(solution)/shard_map/ppermute | solution.py:402
  80.6 2.0 %collective-permute-done.5.first_ref = bf16[576,128]{1,0:T(8,128)(2,1)S(1)} collective-permute-done((bf16[576,128]{1,0:T(8,128)(2,1)S(1)}, bf16[576,128]{1,0:T(8,128)(2,1)S(1)}, u32[]{:S(2)}, u32[]{:S(2)}) %collective-permute-start.5) | collective-permute-done | bytes 147488 | tf_op jit(solution)/shard_map/ppermute | solution.py:402
  82.6 11.0 %collective-permute-done.6.second_ref = bf16[576,128]{1,0:T(8,128)(2,1)S(1)} collective-permute-done((bf16[576,128]{1,0:T(8,128)(2,1)S(1)}, bf16[576,128]{1,0:T(8,128)(2,1)S(1)}, u32[]{:S(2)}, u32[]{:S(2)}) %collective-permute-start.6) | collective-permute-done | bytes 147488 | tf_op jit(solution)/shard_map/ppermute | solution.py:402
  93.7 1.9 %collective-permute-start.7 = (bf16[3,576,128]{2,1,0:T(8,128)(2,1)S(1)}, bf16[3,576,128]{2,1,0:T(8,128)(2,1)S(1)}, u32[]{:S(2)}, u32[]{:S(2)}) collective-permute-start(bf16[3,576,128]{2,1,0:T(8,128)(2,1)S(1)} %shard_map.132.mine_ref), channel_id=1, source_target_pairs={{0,1},{1,0},{48,49},{49,48},{96,97},{97,96},{144,145},{145,144},{2... | collective-permute-start | bytes 1327112 | tf_op jit(solution)/shard_map/ppermute | solution.py:402
  95.6 1.8 %collective-permute-done.7.other_ref = bf16[3,576,128]{2,1,0:T(8,128)(2,1)S(1)} collective-permute-done((bf16[3,576,128]{2,1,0:T(8,128)(2,1)S(1)}, bf16[3,576,128]{2,1,0:T(8,128)(2,1)S(1)}, u32[]{:S(2)}, u32[]{:S(2)}) %collective-permute-start.7) | collective-permute-done | bytes 442400 | tf_op jit(solution)/shard_map/ppermute | solution.py:402
  97.4 2.1 %shard_map.133 = bf16[4,144,1024]{2,1,0:T(8,128)(2,1)} custom-call(bf16[3,576,128]{2,1,0:T(8,128)(2,1)S(1)} %shard_map.132.mine_ref, bf16[3,576,128]{2,1,0:T(8,128)(2,1)S(1)} %collective-permute-done.7.other_ref, bf16[1,768,1024]{2,1,0:T(8,128)(2,1)S(1)} %copy-done.1), custom_call_target="tpu_custom_call" | custom-call | flops 905969664 | bytes 3637248 | tf_op jit(solution)/shard_map/pallas_call | solution.py:59
  99.5 3.7 %all-to-all-start.2 = ((bf16[4,144,1024]{2,1,0:T(8,128)(2,1)}), bf16[4,144,1024]{2,1,0:T(8,128)(2,1)S(1)}, u32[]{:S(2)}, u32[]{:S(2)}) async-start(bf16[4,144,1024]{2,1,0:T(8,128)(2,1)} %shard_map.133), calls=%async_computation.2 | async-start | bytes 2359296 | tf_op jit(solution)/shard_map/all_to_all | solution.py:53
  103.2 3.3 %collective-permute-start.8 = (bf16[1,16,1024]{2,1,0:T(8,128)(2,1)S(1)}, bf16[1,16,1024]{2,1,0:T(8,128)(2,1)S(1)}, u32[]{:S(2)}, u32[]{:S(2)}) collective-permute-start(bf16[1,16,1024]{2,1,0:T(8,128)(2,1)S(1)} %bitcast.4), channel_id=1, source_target_pairs={{0,6},{1,7},{48,54},{49,55},{96,102},{97,103},{144,150},{145,151},... | collective-permute-start | bytes 98312 | tf_op jit(solution)/shard_map/ppermute | solution.py:402
  106.5 3.5 %collective-permute-done.8.b_ref = bf16[1,16,1024]{2,1,0:T(8,128)(2,1)S(1)} collective-permute-done((bf16[1,16,1024]{2,1,0:T(8,128)(2,1)S(1)}, bf16[1,16,1024]{2,1,0:T(8,128)(2,1)S(1)}, u32[]{:S(2)}, u32[]{:S(2)}) %collective-permute-start.8) | collective-permute-done | bytes 32800 | tf_op jit(solution)/shard_map/ppermute | solution.py:402
  110.1 2.4 %collective-permute-start.9 = (bf16[2,16,1024]{2,1,0:T(8,128)(2,1)S(1)}, bf16[2,16,1024]{2,1,0:T(8,128)(2,1)S(1)}, u32[]{:S(2)}, u32[]{:S(2)}) collective-permute-start(bf16[2,16,1024]{2,1,0:T(8,128)(2,1)S(1)} %shard_map.135.a_ref), channel_id=1, source_target_pairs={{0,12},{1,13},{48,60},{49,61},{96,108},{97,109},{144,156},{145,157... | collective-permute-start | bytes 196616 | tf_op jit(solution)/shard_map/ppermute | solution.py:402
  112.5 5.7 %collective-permute-done.9.b_ref = bf16[2,16,1024]{2,1,0:T(8,128)(2,1)S(1)} collective-permute-done((bf16[2,16,1024]{2,1,0:T(8,128)(2,1)S(1)}, bf16[2,16,1024]{2,1,0:T(8,128)(2,1)S(1)}, u32[]{:S(2)}, u32[]{:S(2)}) %collective-permute-start.9) | collective-permute-done | bytes 65568 | tf_op jit(solution)/shard_map/ppermute | solution.py:402
  118.3 6.6 %collective-permute-start.10 = (bf16[4,16,1024]{2,1,0:T(8,128)(2,1)S(1)}, bf16[4,16,1024]{2,1,0:T(8,128)(2,1)S(1)}, u32[]{:S(2)}, u32[]{:S(2)}) collective-permute-start(bf16[4,16,1024]{2,1,0:T(8,128)(2,1)S(1)} %shard_map.136.a_ref), channel_id=1, source_target_pairs={{0,24},{1,25},{48,72},{49,73},{96,120},{97,121},{144,168},{145,169... | collective-permute-start | bytes 393224 | tf_op jit(solution)/shard_map/ppermute | solution.py:402
  124.9 6.8 %collective-permute-done.10.b_ref = bf16[4,16,1024]{2,1,0:T(8,128)(2,1)S(1)} collective-permute-done((bf16[4,16,1024]{2,1,0:T(8,128)(2,1)S(1)}, bf16[4,16,1024]{2,1,0:T(8,128)(2,1)S(1)}, u32[]{:S(2)}, u32[]{:S(2)}) %collective-permute-start.10) | collective-permute-done | bytes 131104 | tf_op jit(solution)/shard_map/ppermute | solution.py:402
  132.2 11.3 %all_to_all.31.in_ref = bf16[4,36,1024]{2,1,0:T(8,128)(2,1)S(1)} all-to-all(bf16[4,36,1024]{2,1,0:T(8,128)(2,1)S(1)} %shard_map.134), channel_id=1, replica_groups=mesh['x'=4,'zl'=4,'y'=8,'zh'=3,'c'=2] {'zl'}, dimensions={0} | all-to-all | bytes 589824 | tf_op jit(solution)/shard_map/all_to_all | solution.py:53
  144.0 14.5 %all_to_all.32.in_ref = bf16[8,16,1152]{2,1,0:T(8,128)(2,1)S(1)} all-to-all(bf16[8,16,1152]{2,1,0:T(8,128)(2,1)S(1)} %shard_map.138), channel_id=1, replica_groups=mesh['x'=4,'zl'=4,'y'=8,'zh'=3,'c'=2] {'y'}, dimensions={0} | all-to-all | bytes 589824 | tf_op jit(solution)/shard_map/all_to_all | solution.py:53
  159.2 7.0 %all-to-all-start.5 = ((f32[6,1,128]{2,1,0:T(1,128)}), f32[6,1,128]{2,1,0:T(1,128)S(1)}, u32[]{:S(2)}, u32[]{:S(2)}) async-start(f32[6,1,128]{2,1,0:T(1,128)} %shard_map.140), calls=%async_computation.5 | async-start | bytes 6144 | tf_op jit(solution)/shard_map/all_to_all | solution.py:53
  166.9 6.3 %all-to-all-done.5.in_ref = f32[6,1,128]{2,1,0:T(1,128)S(1)} async-done(((f32[6,1,128]{2,1,0:T(1,128)}), f32[6,1,128]{2,1,0:T(1,128)S(1)}, u32[]{:S(2)}, u32[]{:S(2)}) %all-to-all-start.5) | async-done | bytes 3104 | tf_op jit(solution)/shard_map/all_to_all | solution.py:53
  (39 shorter events, 6.5 us)
Async XLA Ops:
  4.2 59.9 %collective-permute-start.3 = (bf16[2,3072,128]{2,1,0:T(8,128)(2,1)}, bf16[2,3072,128]{2,1,0:T(8,128)(2,1)S(1)}, u32[]{:S(2)}, u32[]{:S(2)}) collective-permute-start(bf16[2,3072,128]{2,1,0:T(8,128)(2,1)} %get-tuple-element.20), channel_id=1, source_target_pairs={{0,1},{1,0},{48,49},{49,48},{96,97},{97,96},{144,145},{145,144},{2... | collective-permute-start | bytes 4718600 | tf_op jit(solution)/shard_map/ppermute | solution.py:402
  19.5 3.7 %copy-start.9 = (bf16[72,1536]{1,0:T(8,128)(2,1)S(1)}, bf16[72,1536]{1,0:T(8,128)(2,1)}, u32[]{:S(2)}) copy-start(bf16[72,1536]{1,0:T(8,128)(2,1)} %get-tuple-element.15) | copy-start | bytes 663556
  19.6 17.0 %all-to-all-start = ((bf16[4,72,1536]{2,1,0:T(8,128)(2,1)}), bf16[4,72,1536]{2,1,0:T(8,128)(2,1)S(1)}, u32[]{:S(2)}, u32[]{:S(2)}) async-start(bf16[4,72,1536]{2,1,0:T(8,128)(2,1)} %get-tuple-element.14), calls=%async_computation | async-start | bytes 1769472 | tf_op jit(solution)/shard_map/all_to_all | solution.py:53
  23.2 21.5 %collective-permute-start.2 = (bf16[72,1536]{1,0:T(8,128)(2,1)S(1)}, bf16[72,1536]{1,0:T(8,128)(2,1)S(1)}, u32[]{:S(2)}, u32[]{:S(2)}) collective-permute-start(bf16[72,1536]{1,0:T(8,128)(2,1)S(1)} %copy-done.9), channel_id=1, source_target_pairs={{0,96},{1,97},{48,144},{49,145},{96,2},{97,3},{144,50},{145,51},{2... | collective-permute-start | bytes 663560 | tf_op jit(solution)/shard_map/ppermute | solution.py:402
  37.2 24.2 %collective-permute-start = (bf16[144,3072]{1,0:T(8,128)(2,1)S(1)}, bf16[144,3072]{1,0:T(8,128)(2,1)S(1)}, u32[]{:S(2)}, u32[]{:S(2)}) collective-permute-start(bf16[144,3072]{1,0:T(8,128)(2,1)S(1)} %shard_map.123.a_ref), channel_id=1, source_target_pairs={{0,48},{1,149},{48,96},{49,1},{96,144},{97,49},{144,2},{145,97},{2... | collective-permute-start | bytes 2654216 | tf_op jit(solution)/shard_map/ppermute | solution.py:402
  42.8 21.2 %collective-permute-start.1 = (bf16[144,3072]{1,0:T(8,128)(2,1)S(1)}, bf16[144,3072]{1,0:T(8,128)(2,1)S(1)}, u32[]{:S(2)}, u32[]{:S(2)}) collective-permute-start(bf16[144,3072]{1,0:T(8,128)(2,1)S(1)} %shard_map.123.a_ref), channel_id=1, source_target_pairs={{0,148},{1,49},{48,0},{49,97},{96,48},{97,145},{144,96},{145,3},{2... | collective-permute-start | bytes 2654216 | tf_op jit(solution)/shard_map/ppermute | solution.py:402
  44.8 15.1 %copy-start = (bf16[2,3072,128]{2,1,0:T(8,128)(2,1)S(1)}, bf16[2,3072,128]{2,1,0:T(8,128)(2,1)}, u32[]{:S(2)}) copy-start(bf16[2,3072,128]{2,1,0:T(8,128)(2,1)} %get-tuple-element.16.w_ref) | copy-start | bytes 4718596
  67.0 3.9 %collective-permute-start.4 = (f32[576,256]{1,0:T(8,128)S(1)}, f32[576,256]{1,0:T(8,128)S(1)}, u32[]{:S(2)}, u32[]{:S(2)}) collective-permute-start(f32[576,256]{1,0:T(8,128)S(1)} %shard_map.130), channel_id=1, source_target_pairs={{0,1},{1,0},{48,49},{49,48},{96,97},{97,96},{144,145},{145,144},{2... | collective-permute-start | bytes 1769480 | tf_op jit(solution)/shard_map/ppermute | solution.py:402
  70.5 26.9 %copy-start.1 = (bf16[1,768,1024]{2,1,0:T(8,128)(2,1)S(1)}, bf16[1,768,1024]{2,1,0:T(8,128)(2,1)}, u32[]{:S(2)}) copy-start(bf16[1,768,1024]{2,1,0:T(8,128)(2,1)} %w_ref.1) | copy-start | bytes 4718596
  71.4 11.2 %collective-permute-start.5 = (bf16[576,128]{1,0:T(8,128)(2,1)S(1)}, bf16[576,128]{1,0:T(8,128)(2,1)S(1)}, u32[]{:S(2)}, u32[]{:S(2)}) collective-permute-start(bf16[576,128]{1,0:T(8,128)(2,1)S(1)} %shard_map.131.own_ref), channel_id=1, source_target_pairs={{0,2},{1,5},{48,50},{49,53},{96,98},{97,101},{144,146},{145,149},{... | collective-permute-start | bytes 442376 | tf_op jit(solution)/shard_map/ppermute | solution.py:402
  76.2 17.4 %collective-permute-start.6 = (bf16[576,128]{1,0:T(8,128)(2,1)S(1)}, bf16[576,128]{1,0:T(8,128)(2,1)S(1)}, u32[]{:S(2)}, u32[]{:S(2)}) collective-permute-start(bf16[576,128]{1,0:T(8,128)(2,1)S(1)} %shard_map.131.own_ref), channel_id=1, source_target_pairs={{0,4},{1,3},{48,52},{49,51},{96,100},{97,99},{144,148},{145,147},{... | collective-permute-start | bytes 442376 | tf_op jit(solution)/shard_map/ppermute | solution.py:402
  93.7 3.7 %collective-permute-start.7 = (bf16[3,576,128]{2,1,0:T(8,128)(2,1)S(1)}, bf16[3,576,128]{2,1,0:T(8,128)(2,1)S(1)}, u32[]{:S(2)}, u32[]{:S(2)}) collective-permute-start(bf16[3,576,128]{2,1,0:T(8,128)(2,1)S(1)} %shard_map.132.mine_ref), channel_id=1, source_target_pairs={{0,1},{1,0},{48,49},{49,48},{96,97},{97,96},{144,145},{145,144},{2... | collective-permute-start | bytes 1327112 | tf_op jit(solution)/shard_map/ppermute | solution.py:402
  99.5 3.7 %copy-start.2 = (bf16[16,1024]{1,0:T(8,128)(2,1)S(1)}, bf16[16,1024]{1,0:T(8,128)(2,1)}, u32[]{:S(2)}) copy-start(bf16[16,1024]{1,0:T(8,128)(2,1)} %own_ref.1) | copy-start | bytes 98308
  99.5 32.3 %all-to-all-start.2 = ((bf16[4,144,1024]{2,1,0:T(8,128)(2,1)}), bf16[4,144,1024]{2,1,0:T(8,128)(2,1)S(1)}, u32[]{:S(2)}, u32[]{:S(2)}) async-start(bf16[4,144,1024]{2,1,0:T(8,128)(2,1)} %shard_map.133), calls=%async_computation.2 | async-start | bytes 2359296 | tf_op jit(solution)/shard_map/all_to_all | solution.py:53
  103.2 40.4 %copy-start.3 = (bf16[16,1024]{1,0:T(8,128)(2,1)S(1)}, bf16[16,1024]{1,0:T(8,128)(2,1)}, u32[]{:S(2)}) copy-start(bf16[16,1024]{1,0:T(8,128)(2,1)} %get-tuple-element.25.res_ref) | copy-start | bytes 98308
  103.2 40.4 %copy-start.4 = (f32[128,128]{1,0:T(8,128)S(1)}, f32[128,128]{1,0:T(8,128)}, u32[]{:S(2)}) copy-start(f32[128,128]{1,0:T(8,128)} %get-tuple-element.23.gate_ref) | copy-start | bytes 196612
  103.2 40.4 %copy-start.5 = (bf16[72,128]{1,0:T(8,128)(2,1)S(1)}, bf16[72,128]{1,0:T(8,128)(2,1)}, u32[]{:S(2)}) copy-start(bf16[72,128]{1,0:T(8,128)(2,1)} %get-tuple-element.22.place_ref) | copy-start | bytes 55300
  103.2 40.4 %copy-start.6 = (s32[1,128]{1,0:T(1,128)S(1)}, s32[1,128]{1,0:T(1,128)}, u32[]{:S(2)}) copy-start(s32[1,128]{1,0:T(1,128)} %seg_ref.1) | copy-start | bytes 1540
  103.2 6.8 %collective-permute-start.8 = (bf16[1,16,1024]{2,1,0:T(8,128)(2,1)S(1)}, bf16[1,16,1024]{2,1,0:T(8,128)(2,1)S(1)}, u32[]{:S(2)}, u32[]{:S(2)}) collective-permute-start(bf16[1,16,1024]{2,1,0:T(8,128)(2,1)S(1)} %bitcast.4), channel_id=1, source_target_pairs={{0,6},{1,7},{48,54},{49,55},{96,102},{97,103},{144,150},{145,151},... | collective-permute-start | bytes 98312 | tf_op jit(solution)/shard_map/ppermute | solution.py:402
  110.1 8.2 %collective-permute-start.9 = (bf16[2,16,1024]{2,1,0:T(8,128)(2,1)S(1)}, bf16[2,16,1024]{2,1,0:T(8,128)(2,1)S(1)}, u32[]{:S(2)}, u32[]{:S(2)}) collective-permute-start(bf16[2,16,1024]{2,1,0:T(8,128)(2,1)S(1)} %shard_map.135.a_ref), channel_id=1, source_target_pairs={{0,12},{1,13},{48,60},{49,61},{96,108},{97,109},{144,156},{145,157... | collective-permute-start | bytes 196616 | tf_op jit(solution)/shard_map/ppermute | solution.py:402
  118.3 13.5 %collective-permute-start.10 = (bf16[4,16,1024]{2,1,0:T(8,128)(2,1)S(1)}, bf16[4,16,1024]{2,1,0:T(8,128)(2,1)S(1)}, u32[]{:S(2)}, u32[]{:S(2)}) collective-permute-start(bf16[4,16,1024]{2,1,0:T(8,128)(2,1)S(1)} %shard_map.136.a_ref), channel_id=1, source_target_pairs={{0,24},{1,25},{48,72},{49,73},{96,120},{97,121},{144,168},{145,169... | collective-permute-start | bytes 393224 | tf_op jit(solution)/shard_map/ppermute | solution.py:402
  132.2 41.0 %copy-start.7 = (s32[1,4]{1,0:T(1,128)S(1)}, s32[1,4]{1,0:T(1,128)}, u32[]{:S(2)}) copy-start(s32[1,4]{1,0:T(1,128)} %slot_ref.1) | copy-start | bytes 52
  132.2 41.0 %copy-start.8 = (f32[1,4]{1,0:T(1,128)S(1)}, f32[1,4]{1,0:T(1,128)}, u32[]{:S(2)}) copy-start(f32[1,4]{1,0:T(1,128)} %ref_ref.1) | copy-start | bytes 52
  159.2 14.0 %all-to-all-start.5 = ((f32[6,1,128]{2,1,0:T(1,128)}), f32[6,1,128]{2,1,0:T(1,128)S(1)}, u32[]{:S(2)}, u32[]{:S(2)}) async-start(f32[6,1,128]{2,1,0:T(1,128)} %shard_map.140), calls=%async_computation.5 | async-start | bytes 6144 | tf_op jit(solution)/shard_map/all_to_all | solution.py:53
